TPU v7x, 128 devices: a whole 4x4x4 slice. The times are simulated.
128 devices in a mesh: teach: 2 (over core), dp: 64 (over x, z, y).
Axes of the slice: x: 4, y: 4, z: 4, core: 2. Of those that a mesh axis runs over, the one named last changes fastest.
Arguments:
- teacher_logits: bfloat16 [2, 16384, 5000], P('teach', 'dp'), may hold values from -18 to 400
- routes: int32 [16384, 1], P('dp'), may hold values from 0 to 127; in each aligned block of 256 rows (0 to 255, 256 to 511, ...) at most 4 rows name the same one
- agreement: int32 [16384], P('dp'), may hold values 0 or 1
- targets: int32 [16384], P('dp'), may hold values from 0 to 4999
- lengths: int32 [64], P('dp'), may hold values from 64 to 256
- student_hidden: bfloat16 [32768, 1024], P(('teach', 'dp')), may hold values from -6 to 6
- out_weight: bfloat16 [1024, 5000], replicated, may hold values from -2 to 2
- out_bias: float32 [5000], replicated, may hold values from -6 to 6
- gain: float32 [1024], replicated, may hold values from 0.5 to 1.5
Outputs:
- weight_grad: float32 [1024, 5000], P(('teach', 'dp'))
- gain_grad: float32 [1024], replicated
- bias_grad: float32 [5000], replicated
- loss: float32 [], replicated
Inputs may be any that keep to these rules, and one draw needn't show every extreme that they name: `routes`: within the 256 rows of one index of dp, each student device is named at most 4 times, and some device exactly 4 times.
All inputs are finite; a program needn't handle non-finite values. No bound on the sum of `agreement` on one device may be relied on, other than what follows from the above.
Results may differ from a plain program's by a relative error of at most 0.0031.
Values may be sent and summed in bfloat16 or wider, within the bound.
A program may use at most 128 MiB of HBM per device.

v0:
```python
import jax
import jax.numpy as jnp
from jax import lax
from jax.sharding import Mesh
from jax.sharding import PartitionSpec as P

LMAX = 256
DP = ("dp_0", "dp_1", "dp_2")
TEACH_DP = ("teach", "dp_0", "dp_1", "dp_2")


EPSILON = 1e-05


def over_axes(x, axes):
    for axis in axes:
        x = lax.psum(x, axis)
    return x


def route_slots(dest_device, devices):
    onehot = (dest_device[:, None] == jnp.arange(devices, dtype=jnp.int32)[None, :]).astype(
        jnp.float32
    )
    row_ids = jnp.arange(dest_device.shape[0], dtype=jnp.int32)
    earlier = (row_ids[None, :] < row_ids[:, None]).astype(jnp.float32)
    before = jnp.dot(
        earlier, onehot, preferred_element_type=jnp.float32, precision=lax.Precision.HIGHEST
    )
    return jnp.sum(before * onehot, axis=1).astype(jnp.int32)


def live_mask(lengths_block, row_total):
    row_ids = jnp.arange(row_total, dtype=jnp.int32)
    utterance = row_ids // LMAX
    frame_pos = row_ids % LMAX
    picks = utterance[:, None] == jnp.arange(lengths_block.shape[0], dtype=jnp.int32)[None, :]
    row_length = jnp.sum(jnp.where(picks, lengths_block[None, :], 0), axis=1)
    return (frame_pos < row_length).astype(jnp.float32)


def soft_targets(teacher_rows, agree_rows, target_rows, live_rows):
    probs_teacher = jax.nn.softmax(teacher_rows.astype(jnp.float32), axis=-1)
    onehot = (
        target_rows[:, None] == jnp.arange(probs_teacher.shape[1], dtype=jnp.int32)[None, :]
    ).astype(jnp.float32)
    weight = (0.5 * agree_rows.astype(jnp.float32))[:, None]
    return (live_rows[:, None] * (weight * probs_teacher + 0.5 * onehot)).astype(jnp.bfloat16)


def student_forward(hidden_rows, gain, out_weight, out_bias):
    states = hidden_rows.astype(jnp.float32)
    centre = jnp.mean(states, axis=1, keepdims=True)
    spread = jnp.mean(jnp.square(states - centre), axis=1, keepdims=True)
    normed = (states - centre) * lax.rsqrt(spread + EPSILON)
    scaled = (normed * gain[None, :]).astype(jnp.bfloat16)
    logits = jnp.dot(scaled, out_weight, preferred_element_type=jnp.float32) + out_bias[None, :]
    return (normed, scaled, jax.nn.log_softmax(logits, axis=-1))


def combined_grads(first_soft, second_soft, log_probs):
    first_float = first_soft.astype(jnp.float32)
    second_float = second_soft.astype(jnp.float32)
    row_mass = jnp.sum(first_float + second_float, axis=1, keepdims=True)
    return (row_mass * jnp.exp(log_probs) - first_float - second_float).astype(jnp.bfloat16)


def body(
    teacher_logits, routes, agreement, targets, lengths, student_hidden, out_weight, out_bias, gain
):
    teach_count = lax.axis_size("teach")
    data_count = lax.axis_size(DP)
    devices = teach_count * data_count
    rows_here = teacher_logits.shape[1]
    most_slots = 2 * rows_here // devices
    vocab = teacher_logits.shape[2]
    width = student_hidden.shape[1]
    dest_device = routes[:, 0]
    slot_index = route_slots(dest_device, devices)
    live_rows = live_mask(lengths, rows_here)
    soft_rows = soft_targets(teacher_logits[0], agreement, targets, live_rows)
    half = rows_here // 2
    first_here = lax.axis_index("teach") * half
    count_term = jnp.sum(lax.dynamic_slice_in_dim(live_rows, first_here, half, 0))
    stacked = soft_rows.reshape(2, half, vocab)
    both_soft = lax.all_to_all(stacked, "teach", split_axis=0, concat_axis=0, tiled=True)
    dest_half = lax.dynamic_slice_in_dim(dest_device, first_here, half, 0)
    slot_half = lax.dynamic_slice_in_dim(slot_index, first_here, half, 0)
    replicated = jnp.broadcast_to(
        student_hidden.reshape(1, data_count, most_slots, width),
        (teach_count, data_count, most_slots, width),
    ).reshape(devices, most_slots, width)
    arrived = lax.all_to_all(replicated, TEACH_DP, split_axis=0, concat_axis=0, tiled=True)
    hidden_rows = arrived[dest_half, slot_half]
    norm_rows, state_rows, log_probs = student_forward(hidden_rows, gain, out_weight, out_bias)
    grad_rows = combined_grads(both_soft[0], both_soft[1], log_probs)
    loss_term = -jnp.sum(
        (both_soft[0].astype(jnp.float32) + both_soft[1].astype(jnp.float32)) * log_probs
    )
    back_rows = lax.dot_general(
        grad_rows, out_weight, (((1,), (1,)), ((), ())), preferred_element_type=jnp.float32
    )
    gain_grad = jnp.sum(back_rows * norm_rows, axis=0)
    bias_grad = jnp.sum(grad_rows.astype(jnp.float32), axis=0)
    weight_grad = lax.psum_scatter(
        lax.dot_general(
            state_rows, grad_rows, (((0,), (0,)), ((), ())), preferred_element_type=jnp.float32
        ),
        TEACH_DP,
        scatter_dimension=0,
        tiled=True,
    )
    gain_sum, bias_sum, loss_sum, total_frames = (
        over_axes(gain_grad, TEACH_DP),
        over_axes(bias_grad, TEACH_DP),
        over_axes(loss_term, TEACH_DP),
        over_axes(count_term, TEACH_DP),
    )
    inverse = 1.0 / total_frames
    return (weight_grad * inverse, gain_sum * inverse, bias_sum * inverse, loss_sum * inverse)


def solution(mesh):
    finer = Mesh(
        mesh.devices.reshape(mesh.shape["teach"], 4, 4, 4), ("teach", "dp_0", "dp_1", "dp_2")
    )
    in_specs = (
        P("teach", DP, None),
        P(DP, None),
        P(DP),
        P(DP),
        P(DP),
        P(TEACH_DP, None),
        P(),
        P(),
        P(),
    )
    out_specs = (P(TEACH_DP, None), P(), P(), P())
    return jax.shard_map(body, mesh=finer, in_specs=in_specs, out_specs=out_specs, check_vma=False)
```

profile of v0, /device:TPU:1, one launch (start us, length us, event | category | flops | bytes accessed | tf_op | source)
XLA Modules:
  0.0 783.0 jit_solution(15204521626412033606)
XLA Ops:
  7.2 1.4 broadcast_in_dim.22
  8.6 1.2 broadcast_in_dim.23
  9.8 11.9 %all-to-all-start = ((bf16[128,4,1024]{2,1,0:T(4,128)(2,1)}), bf16[128,4,1024]{2,1,0:T(4,128)(2,1)}, u32[]{:S(2)}, u32[]{:S(2)}) async-start(bf16[128,4,1024]{2,1,0:T(4,128)(2,1)} %bitcast.51), calls=%async_computation | async-start | bytes 2097152 | tf_op jit(solution)/shard_map/all_to_all | solution.py:93
  22.4 4.0 copy.13
  26.4 0.7 reduce_max.28
  27.1 0.0 copy-done.7
  27.1 0.2 fusion.5
  27.4 0.9 fusion.1
  28.3 5.9 copy.14
  34.2 0.1 fusion.18
  34.3 5.7 multiply_convert_fusion
  40.0 6.1 all-to-all-start.1
  46.1 2.3 gather_fusion
  48.4 0.1 convert_reduce_fusion.1
  48.5 0.2 fusion.10
  48.7 6.3 fusion.23
  55.1 0.7 exponential_reduce_fusion
  55.8 3.0 multiply_reduce_fusion
  58.8 2.7 convert_reduce_fusion
  61.5 1.0 copy-done.1
  62.5 8.7 %fusion.19 = f32[1024,5000]{1,0:T(8,128)} fusion(bf16[128,5000]{0,1:T(8,128)(2,1)S(1)} %get-tuple-element.23, bf16[128,1024]{1,0:T(8,128)(2,1)S(1)} %gather_fusion, f32[1024]{0:T(1024)S(1)} %copy-done.3, f32[128]{0:T(128)S(1)} %add_rsqrt_fusion, f32[128]{0:T(128)S(1)} %broadcast_multiply_fusion.3), kind=kOutput, calls=%fused_computation.58 | convolution fusion | flops 1311375360 | bytes 22027264 | tf_op jit(solution)/shard_map/dot_general | solution.py:106
  71.2 0.0 reduce-scatter.2.cloned.1.call-update
  71.2 0.7 dynamic-slice_reduce_fusion
  72.5 5.6 fusion.4
  78.2 4.6 all-reduce.3
  82.8 14.6 %all-reduce.2 = (f32[]{:T(128)}, f32[1024]{0:T(1024)S(1)}, f32[5000]{0:T(1024)S(1)}, f32[]{:T(128)}) all-reduce(f32[]{:T(128)} %get-tuple-element.18, f32[1024]{0:T(1024)S(1)} %get-tuple-element.19, f32[5000]{0:T(1024)S(1)} %get-tuple-element.20, f32[]{:T(128)} %get-tuple-element.21), channel_id=1, replica_groups=mesh['teach'=2,'dp_0'=4,'dp_1'=4,'dp_2'=4] {'dp_0'}, use_global_device_ids=true, to_apply=%region_11.12 | all-reduce | flops 6026 | bytes 48208 | tf_op jit(solution)/shard_map/psum | solution.py:17
  97.4 16.3 %all-reduce.1 = (f32[]{:T(128)}, f32[1024]{0:T(1024)S(1)}, f32[5000]{0:T(1024)S(1)}, f32[]{:T(128)}) all-reduce(f32[]{:T(128)} %get-tuple-element.14, f32[1024]{0:T(1024)S(1)} %get-tuple-element.15, f32[5000]{0:T(1024)S(1)} %get-tuple-element.16, f32[]{:T(128)} %get-tuple-element.17), channel_id=1, replica_groups=mesh['teach'=2,'dp_0'=4,'dp_1'=4,'dp_2'=4] {'dp_1'}, use_global_device_ids=true, to_apply=%region_12.13 | all-reduce | flops 6026 | bytes 48208 | tf_op jit(solution)/shard_map/psum | solution.py:17
  113.6 15.8 %all-reduce = (f32[]{:T(128)}, f32[1024]{0:T(1024)S(1)}, f32[5000]{0:T(1024)S(1)}, f32[]{:T(128)}) all-reduce(f32[]{:T(128)} %get-tuple-element.10, f32[1024]{0:T(1024)S(1)} %get-tuple-element.11, f32[5000]{0:T(1024)S(1)} %get-tuple-element.12, f32[]{:T(128)} %get-tuple-element.13), channel_id=1, replica_groups=mesh['teach'=2,'dp_0'=4,'dp_1'=4,'dp_2'=4] {'dp_2'}, use_global_device_ids=true, to_apply=%region_13.14 | all-reduce | flops 6026 | bytes 48208 | tf_op jit(solution)/shard_map/psum | solution.py:17
  130.8 0.6 broadcast_multiply_fusion.2
  131.4 0.6 broadcast_multiply_fusion.1
  132.0 641.4 %reduce-scatter.2.cloned.1.call-done = f32[8,5000]{1,0:T(8,128)} async-done(((f32[1024,5000]{1,0:T(8,128)}), f32[8,5000]{1,0:T(8,128)}) %reduce-scatter.2.cloned.1.call-update) | async-done | bytes 160016 | tf_op jit(solution)/shard_map/reduce_scatter | solution.py:105
  773.4 1.6 broadcast_multiply_fusion
  (25 shorter events, 0.1 us)
Async XLA Ops:
  7.2 15.3 %copy-start = (bf16[1,256,5000]{1,2,0:T(8,128)(2,1)S(1)}, bf16[1,256,5000]{1,2,0:T(8,128)(2,1)}, u32[]{:S(2)}) copy-start(bf16[1,256,5000]{1,2,0:T(8,128)(2,1)} %param.9) | copy-start | bytes 7680004
  9.8 30.2 %all-to-all-start = ((bf16[128,4,1024]{2,1,0:T(4,128)(2,1)}), bf16[128,4,1024]{2,1,0:T(4,128)(2,1)}, u32[]{:S(2)}, u32[]{:S(2)}) async-start(bf16[128,4,1024]{2,1,0:T(4,128)(2,1)} %bitcast.51), calls=%async_computation | async-start | bytes 2097152 | tf_op jit(solution)/shard_map/all_to_all | solution.py:93
  26.4 0.7 copy-start.6
  26.4 0.7 copy-start.7
  28.3 6.0 copy-start.5
  40.0 15.8 %all-to-all-start.1 = ((bf16[2,128,5000]{1,2,0:T(8,128)(2,1)}), bf16[2,128,5000]{1,2,0:T(8,128)(2,1)}, u32[]{:S(2)}, u32[]{:S(2)}) async-start(bf16[2,128,5000]{1,2,0:T(8,128)(2,1)} %multiply_convert_fusion), calls=%async_computation.1 | async-start | bytes 5120000 | tf_op jit(solution)/shard_map/all_to_all | solution.py:86
  46.1 2.6 copy-start.3
  46.1 2.6 copy-start.4
  46.1 727.3 %reduce-scatter.2.cloned.1.call-start = ((), (), s32[]{:S(2)}) async-start(), calls=%async_computation.3 | async-start | bytes 21135360 | tf_op jit(solution)/shard_map/reduce_scatter | solution.py:105
  61.5 1.0 copy-start.1
  71.2 1.4 copy-start.2
Sparse Core Ops, SparseCore 0:
  71.3 702.0 reduce-scatter.1
where the time goes:
time: 784 us; the launch traced here: 783 us
  waiting for transfers between devices  641 us (82%)
  blocking collectives  51.3 us (7%)
  matrix products  20.9 us (3%)
  starting transfers between devices  18.1 us (2%)
  between operations  17.9 us (2%)
  other arithmetic  17.5 us (2%)
  local copies, waits for them, and re-layouts  15.9 us (2%)
    reduce_scatter x1, waiting for transfers between devices, body(): lax.psum_scatter(lax.dot_general(state_rows, grad_rows, (((0,), (0,)), ((...  641 us
    psum x4, blocking collectives, over_axes(): x = lax.psum(x, axis)  51.3 us
  transfers between devices with their start and end apart: 3, of which 1 were waited for; matrix products, arithmetic and copies ran while one was open for 4% of the time, Pallas kernels for 0%

commit v1 on v0

--- a/solution.py
+++ b/solution.py
@@ -1,21 +1,25 @@
 import jax
 import jax.numpy as jnp
 from jax import lax
+from jax.experimental import pallas as pl
+from jax.experimental.pallas import tpu as pltpu
 from jax.sharding import Mesh
 from jax.sharding import PartitionSpec as P
 
 LMAX = 256
 DP = ("dp_0", "dp_1", "dp_2")
 TEACH_DP = ("teach", "dp_0", "dp_1", "dp_2")
-
+MESH = pl.DeviceIdType.MESH
 
 EPSILON = 1e-05
 
-
-def over_axes(x, axes):
-    for axis in axes:
-        x = lax.psum(x, axis)
-    return x
+HALF_V = 2560
+THIRDS = ((0, 896), (896, 896), (1792, 768))
+WIDEST = 896
+STAGE_ROWS = (256, 128, 64, 32, 16, 8)
+STAGE_AT = (0, 256, 384, 448, 480, 496)
+PARTS = 6
+STAGES = 6
 
 
 def route_slots(dest_device, devices):
@@ -63,6 +67,207 @@
     second_float = second_soft.astype(jnp.float32)
     row_mass = jnp.sum(first_float + second_float, axis=1, keepdims=True)
     return (row_mass * jnp.exp(log_probs) - first_float - second_float).astype(jnp.bfloat16)
+
+
+def chunk_of(part, row):
+    bits = [0] * 6
+    for k in range(6):
+        bits[(part + k) % 6] = (row >> (5 - k)) & 1
+    chip = 0
+    for dim in range(3):
+        low, high = bits[dim], bits[3 + dim]
+        chip = chip * 4 + high * 2 + (high ^ low)
+    return chip
+
+
+def reduce_kernel(
+    scaled_ref, grad_ref, vec_ref, out_ref, vec_out_ref,
+    lhs, acc, sent, got, sent_last, got_last, final, final_in, vec, vec_in,
+    send_sem, recv_sem, vec_send_sem, vec_recv_sem, final_send_sem, final_recv_sem,
+):
+    t = lax.axis_index("teach")
+    place = [lax.axis_index(axis) for axis in DP]
+
+    def partner(bit):
+        ids = list(place)
+        v = place[bit % 3]
+        ids[bit % 3] = (3 - v) if bit >= 3 else (v + 1 - 2 * (v % 2))
+        return (t, ids[0], ids[1], ids[2])
+
+    def my_bit(bit):
+        v = place[bit % 3]
+        return v // 2 if bit >= 3 else (v // 2 + v % 2) % 2
+
+    partners = [partner(bit) for bit in range(6)]
+    mine = [my_bit(bit) for bit in range(6)]
+    other_core = (1 - t, place[0], place[1], place[2])
+
+    barrier = pltpu.get_barrier_semaphore()
+    for device in partners + [other_core]:
+        pl.semaphore_signal(barrier, inc=1, device_id=device, device_id_type=MESH)
+
+    for part in range(PARTS):
+        half = part // 3
+        for row in range(0, 64, 2):
+            pair = jnp.concatenate(
+                [scaled_ref[half * 64 + chunk_of(part, row)], scaled_ref[half * 64 + chunk_of(part, row + 1)]],
+                axis=0,
+            )
+            lhs[part, row * 8:row * 8 + 16, :] = pair.astype(jnp.bfloat16)
+
+    pl.semaphore_wait(barrier, 7)
+
+    def copy_of(part, stage):
+        width = THIRDS[part % 3][1]
+        if stage == STAGES - 1:
+            source = sent_last.at[part, :, 0:width]
+            target = got_last.at[part, :, 0:width]
+        else:
+            rows = slice(STAGE_AT[stage], STAGE_AT[stage] + STAGE_ROWS[stage])
+            source = sent.at[part, rows, 0:width]
+            target = got.at[part, rows, 0:width]
+        return pltpu.make_async_remote_copy(
+            src_ref=source,
+            dst_ref=target,
+            send_sem=send_sem.at[part * STAGES + stage],
+            recv_sem=recv_sem.at[part * STAGES + stage],
+            device_id=partners[(part + stage) % 6],
+            device_id_type=MESH,
+        )
+
+    def vec_copy(stage):
+        return pltpu.make_async_remote_copy(
+            src_ref=vec.at[stage],
+            dst_ref=vec_in.at[stage],
+            send_sem=vec_send_sem.at[stage],
+            recv_sem=vec_recv_sem.at[stage],
+            device_id=partners[stage] if stage < STAGES else other_core,
+            device_id_type=MESH,
+        )
+
+    vec[0] = vec_ref[...]
+    vec_copy(0).start()
+
+    for part in range(PARTS):
+        first, width = THIRDS[part % 3]
+        away = pl.multiple_of((1 - mine[part]) * 256, 256)
+        block = jnp.dot(
+            lhs[part, pl.ds(away, 256), :], grad_ref[:, first:first + width],
+            preferred_element_type=jnp.float32,
+        )
+        sent[part, 0:256, 0:width] = block.astype(jnp.bfloat16)
+        copy_of(part, 0).start()
+    for part in range(PARTS):
+        first, width = THIRDS[part % 3]
+        stay = pl.multiple_of(mine[part] * 256, 256)
+        acc[part, :, 0:width] = jnp.dot(
+            lhs[part, pl.ds(stay, 256), :], grad_ref[:, first:first + width],
+            preferred_element_type=jnp.float32,
+        )
+
+    base = [0] * PARTS
+    for stage in range(1, STAGES):
+        rows = STAGE_ROWS[stage]
+        before = STAGE_AT[stage - 1]
+        for part in range(PARTS):
+            width = THIRDS[part % 3][1]
+            bit = mine[(part + stage) % 6]
+            away, stay = (1 - bit) * rows, bit * rows
+            copy_of(part, stage - 1).wait_recv()
+            if stage < STAGES - 1:
+                at = pl.multiple_of(base[part] + away, 16)
+                block = acc[part, pl.ds(at, rows), 0:width] + got[
+                    part, pl.ds(pl.multiple_of(before + away, 16), rows), 0:width
+                ].astype(jnp.float32)
+                sent[part, STAGE_AT[stage]:STAGE_AT[stage] + rows, 0:width] = block.astype(jnp.bfloat16)
+                copy_of(part, stage).start()
+                at = pl.multiple_of(base[part] + stay, 16)
+                acc[part, pl.ds(at, rows), 0:width] += got[
+                    part, pl.ds(pl.multiple_of(before + stay, 16), rows), 0:width
+                ].astype(jnp.float32)
+            else:
+                at = pl.multiple_of(base[part] + 0, 16)
+                acc[part, pl.ds(at, 2 * rows), 0:width] += got[
+                    part, before:before + 2 * rows, 0:width
+                ].astype(jnp.float32)
+                at = pl.multiple_of(base[part] + away, 8)
+                sent_last[part, :, 0:width] = acc[part, pl.ds(at, rows), 0:width]
+                copy_of(part, stage).start()
+            base[part] = base[part] + stay
+        vec_copy(stage - 1).wait_recv()
+        vec[stage] = vec[stage - 1] + vec_in[stage - 1]
+        vec_copy(stage).start()
+
+    vec_copy(STAGES - 1).wait_recv()
+    vec[STAGES] = vec[STAGES - 1] + vec_in[STAGES - 1]
+    vec_copy(STAGES).start()
+    for part in range(PARTS):
+        first, width = THIRDS[part % 3]
+        copy_of(part, STAGES - 1).wait_recv()
+        at = pl.multiple_of(base[part], 8)
+        final[part // 3, :, first:first + width] = (
+            acc[part, pl.ds(at, 8), 0:width] + got_last[part, :, 0:width]
+        )
+
+    swap = pltpu.make_async_remote_copy(
+        src_ref=final.at[1 - t],
+        dst_ref=final_in,
+        send_sem=final_send_sem,
+        recv_sem=final_recv_sem,
+        device_id=other_core,
+        device_id_type=MESH,
+    )
+    swap.start()
+    out_ref[t] = final[t]
+    vec_out_ref[t] = vec[STAGES]
+    vec_copy(STAGES).wait_recv()
+    vec_out_ref[1 - t] = vec_in[STAGES]
+    swap.wait_recv()
+    out_ref[1 - t] = final_in[...]
+
+    for part in range(PARTS):
+        for stage in range(STAGES):
+            copy_of(part, stage).wait_send()
+    for stage in range(STAGES + 1):
+        vec_copy(stage).wait_send()
+    swap.wait_send()
+
+
+def reduce_grads(scaled_t, grad, vec):
+    rows = scaled_t.shape[-1]
+    vmem = pl.BlockSpec(memory_space=pltpu.VMEM)
+    buffer_rows = STAGE_AT[-1]
+    dma = pltpu.SemaphoreType.DMA
+    return pl.pallas_call(
+        reduce_kernel,
+        out_shape=(
+            jax.ShapeDtypeStruct((2, 8, HALF_V), jnp.float32),
+            jax.ShapeDtypeStruct((2,) + vec.shape, jnp.float32),
+        ),
+        in_specs=[vmem] * 3,
+        out_specs=(vmem, vmem),
+        scratch_shapes=[
+            pltpu.VMEM((PARTS, 512, rows), jnp.bfloat16),
+            pltpu.VMEM((PARTS, 256, WIDEST), jnp.float32),
+            pltpu.VMEM((PARTS, buffer_rows, WIDEST), jnp.bfloat16),
+            pltpu.VMEM((PARTS, buffer_rows, WIDEST), jnp.bfloat16),
+            pltpu.VMEM((PARTS, 8, WIDEST), jnp.float32),
+            pltpu.VMEM((PARTS, 8, WIDEST), jnp.float32),
+            pltpu.VMEM((2, 8, HALF_V), jnp.float32),
+            pltpu.VMEM((8, HALF_V), jnp.float32),
+            pltpu.VMEM((STAGES + 1,) + vec.shape, jnp.float32),
+            pltpu.VMEM((STAGES + 1,) + vec.shape, jnp.float32),
+            dma((PARTS * STAGES,)),
+            dma((PARTS * STAGES,)),
+            dma((STAGES + 1,)),
+            dma((STAGES + 1,)),
+            dma,
+            dma,
+        ],
+        compiler_params=pltpu.CompilerParams(
+            collective_id=0, has_side_effects=True, vmem_limit_bytes=48 * 1024 * 1024
+        ),
+    )(scaled_t, grad, vec)
 
 
 def body(
@@ -101,23 +306,31 @@
         grad_rows, out_weight, (((1,), (1,)), ((), ())), preferred_element_type=jnp.float32
     )
     gain_grad = jnp.sum(back_rows * norm_rows, axis=0)
-    bias_grad = jnp.sum(grad_rows.astype(jnp.float32), axis=0)
-    weight_grad = lax.psum_scatter(
-        lax.dot_general(
-            state_rows, grad_rows, (((0,), (0,)), ((), ())), preferred_element_type=jnp.float32
-        ),
-        TEACH_DP,
-        scatter_dimension=0,
-        tiled=True,
-    )
-    gain_sum, bias_sum, loss_sum, total_frames = (
-        over_axes(gain_grad, TEACH_DP),
-        over_axes(bias_grad, TEACH_DP),
-        over_axes(loss_term, TEACH_DP),
-        over_axes(count_term, TEACH_DP),
-    )
-    inverse = 1.0 / total_frames
-    return (weight_grad * inverse, gain_sum * inverse, bias_sum * inverse, loss_sum * inverse)
+
+    padded = jnp.pad(grad_rows, ((0, 0), (0, 2 * HALF_V - vocab)))
+    halves = jnp.swapaxes(padded.reshape(half, 2, HALF_V), 0, 1)
+    grad_half = lax.all_to_all(halves, "teach", split_axis=0, concat_axis=0, tiled=True)
+    grad_half = grad_half.reshape(rows_here, HALF_V)
+    state_all = lax.all_gather(state_rows, "teach", axis=0, tiled=True)
+    bias_grad = jnp.sum(grad_half.astype(jnp.float32), axis=0)
+    scaled_t = state_all.astype(jnp.float32).T.reshape(width // 8, 8, rows_here)
+    vec = jnp.concatenate(
+        [gain_grad, bias_grad, loss_term[None], count_term[None], jnp.zeros((510,), jnp.float32)]
+    ).reshape(8, 512)
+    weight_grad, sums = reduce_grads(scaled_t, grad_half, vec)
+    sums = sums.reshape(2, 4096)
+    both = sums[0] + sums[1]
+    inverse = 1.0 / both[width + HALF_V + 1]
+    weight_grad = jnp.concatenate([weight_grad[0], weight_grad[1]], axis=1)[:, :vocab]
+    bias_sum = jnp.concatenate(
+        [sums[0, width:width + HALF_V], sums[1, width:width + vocab - HALF_V]]
+    )
+    return (
+        weight_grad * inverse,
+        both[:width] * inverse,
+        bias_sum * inverse,
+        both[width + HALF_V] * inverse,
+    )
 
 
 def solution(mesh):

time: 784 us -> 122 us (0.16)
  waiting for transfers between devices: 641 us -> 1.29 us
  blocking collectives: 51.3 us -> 2.36 us
  Pallas kernels: 0 us -> 41.5 us
  between operations: 17.9 us -> 4.64 us
  matrix products: 20.9 us -> 12.1 us
    reduce_scatter x1 -> x0, waiting for transfers between devices: 641 us -> none  [body(): lax.psum_scatter(lax.dot_general(state_rows, grad_rows, (((0,), (0,)), ((...]
    psum x4 -> x0, blocking collectives: 51.3 us -> none  [over_axes(): x = lax.psum(x, axis)]
    pallas_call x0 -> x1, Pallas kernels: none -> 41.5 us  [reduce_grads(): pl.pallas_call(reduce_kernel, out_shape=(jax.ShapeDtypeStruct((2, 8, HALF...]
    dot_general x1 -> x0, matrix products: 8.65 us -> none  [body(): lax.dot_general(state_rows, grad_rows, (((0,), (0,)), ((), ())), preferre...]
  transfers between devices with their start and end apart: 3 -> 3, of which waited for: 1 -> 1; matrix products, arithmetic and copies ran while one was open for 4% -> 23% of each run, Pallas kernels for 0% -> 0%
where the time goes in v1:
time: 122 us; the launch traced here: 121 us
  Pallas kernels  41.5 us (34%)
  starting transfers between devices  21.8 us (18%)
  local copies, waits for them, and re-layouts  19.9 us (16%)
  other arithmetic  17.4 us (14%)
  matrix products  12.1 us (10%)
  between operations  4.64 us (4%)
  blocking collectives  2.36 us (2%)
  waiting for transfers between devices  1.29 us (1%)
    pallas_call x1, Pallas kernels, reduce_grads(): pl.pallas_call(reduce_kernel, out_shape=(jax.ShapeDtypeStruct((2, 8, HALF...  41.5 us
    all_to_all x1, starting transfers between devices, body(): lax.all_to_all(replicated, TEACH_DP, split_axis=0, concat_axis=0, tiled=T...  11.9 us
    convert_element_type x2, local copies, waits for them, and re-layouts, soft_targets(): probs_teacher = jax.nn.softmax(teacher_rows.astype(jnp.float32), axis=-1)  9.89 us
    all_to_all x1, starting transfers between devices, body(): lax.all_to_all(stacked, 'teach', split_axis=0, concat_axis=0, tiled=True)  6.14 us
    dot_general x1, matrix products, student_forward(): jnp.dot(scaled, out_weight, preferred_element_type=jnp.float32)  6.12 us
    dot_general x1, matrix products, body(): lax.dot_general(grad_rows, out_weight, (((1,), (1,)), ((), ())), preferre...  5.74 us
    convert_element_type x1, other arithmetic, soft_targets(): (live_rows[:, None] * (weight * probs_teacher + 0.5 * onehot)).astype(jnp...  5.66 us
    all_to_all x1, starting transfers between devices, body(): lax.all_to_all(halves, 'teach', split_axis=0, concat_axis=0, tiled=True)  3.75 us
  transfers between devices with their start and end apart: 3, of which 1 were waited for; matrix products, arithmetic and copies ran while one was open for 23% of the time, Pallas kernels for 0%

profile of v1, /device:TPU:1, one launch (start us, length us, event | category | flops | bytes accessed | tf_op | source)
XLA Modules:
  0.0 121.1 jit_solution(3220485092024680801)
XLA Ops:
  0.7 1.4 %broadcast_in_dim.28 = bf16[64,4,1024]{2,1,0:T(4,128)(2,1)S(1)} reshape(bf16[256,1024]{1,0:T(8,128)(2,1)} %param.14) | data formatting | bytes 1048576 | tf_op jit(solution)/shard_map/broadcast_in_dim | solution.py:294
  2.0 1.2 %broadcast_in_dim.29 = bf16[2,64,4,1024]{3,2,1,0:T(4,128)(2,1)} broadcast(bf16[64,4,1024]{2,1,0:T(4,128)(2,1)S(1)} %broadcast_in_dim.28), dimensions={1,2,3} | broadcast | bytes 1572864 | tf_op jit(solution)/shard_map/broadcast_in_dim | solution.py:294
  3.3 11.9 %all-to-all-start = ((bf16[128,4,1024]{2,1,0:T(4,128)(2,1)}), bf16[128,4,1024]{2,1,0:T(4,128)(2,1)}, u32[]{:S(2)}, u32[]{:S(2)}) async-start(bf16[128,4,1024]{2,1,0:T(4,128)(2,1)} %bitcast.75), calls=%async_computation | async-start | bytes 2097152 | tf_op jit(solution)/shard_map/all_to_all | solution.py:298
  15.3 0.2 fusion.5
  15.5 4.0 %copy.16 = f32[1,256,5000]{2,1,0:T(8,128)} copy(bf16[1,256,5000]{1,2,0:T(8,128)(2,1)S(1)} %copy-done) | data formatting | bytes 7680000 | tf_op jit(solution)/shard_map/convert_element_type | solution.py:47
  19.5 0.7 reduce_max.28
  20.2 0.9 fusion.1
  21.8 5.9 %copy.17 = f32[2,128,5000]{1,2,0:T(8,128)} copy(f32[2,128,5000]{2,1,0:T(8,128)} %bitcast.73) | data formatting | bytes 10240000 | tf_op jit(solution)/shard_map/convert_element_type | solution.py:47
  27.8 0.7 dynamic-slice_reduce_fusion
  28.5 5.7 %multiply_convert_fusion = bf16[2,128,5000]{1,2,0:T(8,128)(2,1)} fusion(f32[2,128,5000]{1,2,0:T(8,128)} %copy.17, s32[2,128]{1,0:T(2,128)S(1)} %bitcast.81, f32[2,128]{1,0:T(2,128)S(1)} %bitcast.79, f32[2,128]{1,0:T(2,128)S(1)} %get-tuple-element.14, f32[2,128]{1,0:T(2,128)S(1)} %multiply_bitcast_fusion, f32[2,128]{1,0:T(2,128)S(1)} %compare_convert_fusion.1), kind=kLoop, calls=%fused_computation.5 | loop fusion | flops 10240000 | bytes 7685120 | tf_op jit(solution)/shard_map/convert_element_type | solution.py:52
  34.1 6.1 %all-to-all-start.1 = ((bf16[2,128,5000]{1,2,0:T(8,128)(2,1)}), bf16[2,128,5000]{1,2,0:T(8,128)(2,1)}, u32[]{:S(2)}, u32[]{:S(2)}) async-start(bf16[2,128,5000]{1,2,0:T(8,128)(2,1)} %multiply_convert_fusion), calls=%async_computation.1 | async-start | bytes 5120000 | tf_op jit(solution)/shard_map/all_to_all | solution.py:291
  40.3 2.3 %gather_fusion = bf16[128,1024]{1,0:T(8,128)(2,1)S(1)} fusion(bf16[128,4,1024]{2,1,0:T(4,128)(2,1)} %all-to-all-done, s32[128]{0:T(128)S(1)} %fusion.20), kind=kCustom, calls=%fused_computation | custom fusion | bytes 525312 | tf_op jit(solution)/shard_map/gather | solution.py:299
  42.7 0.2 fusion.10
  42.9 0.2 fusion.9
  43.1 2.4 %all_gather.3 = bf16[256,1024]{1,0:T(8,128)(2,1)S(1)} all-gather(bf16[128,1024]{1,0:T(8,128)(2,1)S(1)} %fusion.9), channel_id=1, replica_groups=mesh['teach'=2,'dp_0'=4,'dp_1'=4,'dp_2'=4] {'teach'}, dimensions={0}, use_global_device_ids=true | all-gather | bytes 786432 | tf_op jit(solution)/shard_map/all_gather | solution.py:314
  45.5 6.1 %fusion.22 = (f32[128]{0:T(128)S(1)}, f32[128,5000]{0,1:T(8,128)S(1)}) fusion(f32[5000]{0:T(1024)S(1)} %copy-done.1, bf16[128,1024]{1,0:T(8,128)(2,1)S(1)} %fusion.9, bf16[1024,5000]{0,1:T(8,128)(2,1)} %param.15), kind=kOutput, calls=%fused_computation.67 | convolution fusion | flops 1311999872 | bytes 13082656 | tf_op jit(solution)/shard_map/dot_general | solution.py:61
  51.6 0.7 exponential_reduce_fusion
  52.3 3.0 %multiply_reduce_fusion = (f32[]{:T(128)}, f32[128]{0:T(128)S(1)}) fusion(f32[128,5000]{0,1:T(8,128)S(1)} %get-tuple-element.17, f32[128]{0:T(128)S(1)} %log.9, f32[128]{0:T(128)S(1)} %get-tuple-element.16, bf16[2,128,5000]{1,2,0:T(8,128)(2,1)} %all-to-all-done.1), kind=kLoop, calls=%fused_computation.12 | loop fusion | flops 5119871 | bytes 5121540 | tf_op jit(solution)/shard_map/reduce_sum | solution.py:302
  55.3 2.5 %fusion.2 = bf16[128,5000]{0,1:T(8,128)(2,1)S(1)} fusion(f32[128,5000]{0,1:T(8,128)S(1)} %get-tuple-element.17, f32[128]{0:T(128)S(1)} %log.9, f32[128]{0:T(128)S(1)} %get-tuple-element.16, f32[128]{0:T(128)S(1)} %get-tuple-element.9, bf16[2,128,5000]{1,2,0:T(8,128)(2,1)} %all-to-all-done.1), kind=kLoop, calls=%fused_computation.11 | loop fusion | flops 5120000 | bytes 6401536 | tf_op jit(solution)/shard_map/convert_element_type | solution.py:69
  57.8 5.7 %fusion.4 = f32[1024]{0:T(1024)S(1)} fusion(bf16[128,5000]{0,1:T(8,128)(2,1)S(1)} %fusion.2, bf16[1024,5000]{0,1:T(8,128)(2,1)} %param.15, bf16[128,1024]{1,0:T(8,128)(2,1)S(1)} %gather_fusion, f32[128]{0:T(128)S(1)} %add_rsqrt_fusion, f32[128]{0:T(128)S(1)} %broadcast_multiply_fusion), kind=kOutput, calls=%fused_computation.18 | convolution fusion | flops 1311374336 | bytes 11787264 | tf_op jit(solution)/shard_map/dot_general | solution.py:305
  63.7 1.5 %copy.18 = bf16[128,2,2560]{2,0,1:T(8,128)(2,1)} copy(bf16[128,2,2560]{0,2,1:T(8,128)(2,1)S(1)} %bitcast.74) | data formatting | bytes 2621440 | tf_op jit(solution)/shard_map/reshape | solution.py:311
  65.1 3.7 %all-to-all-start.2 = ((bf16[2,128,2560]{2,1,0:T(8,128)(2,1)}), bf16[2,128,2560]{2,1,0:T(8,128)(2,1)S(1)}, u32[]{:S(2)}, u32[]{:S(2)}) async-start(bf16[2,128,2560]{2,1,0:T(8,128)(2,1)} %bitcast.16), calls=%async_computation.2 | async-start | bytes 2621440 | tf_op jit(solution)/shard_map/all_to_all | solution.py:312
  69.5 1.3 %all-to-all-done.2 = bf16[2,128,2560]{2,1,0:T(8,128)(2,1)S(1)} async-done(((bf16[2,128,2560]{2,1,0:T(8,128)(2,1)}), bf16[2,128,2560]{2,1,0:T(8,128)(2,1)S(1)}, u32[]{:S(2)}, u32[]{:S(2)}) %all-to-all-start.2) | async-done | bytes 1310752 | tf_op jit(solution)/shard_map/all_to_all | solution.py:312
  70.8 0.2 convert_reduce_fusion
  71.0 0.7 concatenate.13
  71.8 1.1 convert_bitcast_fusion
  72.9 1.6 %copy.15 = f32[1024,256]{1,0:T(8,128)S(1)} copy(f32[1024,256]{0,1:T(8,128)} %convert_bitcast_fusion) | data formatting | bytes 2097152 | tf_op jit(solution)/shard_map/reshape | solution.py:316
  74.4 41.5 %shard_map.120 = (f32[2,8,2560]{2,1,0:T(8,128)S(1)}, f32[2,8,512]{2,1,0:T(8,128)S(1)}) custom-call(f32[128,8,256]{2,1,0:T(8,128)S(1)} %bitcast.71, bf16[256,2560]{1,0:T(8,128)(2,1)S(1)} %bitcast.70, f32[8,512]{1,0:T(8,128)S(1)} %reshape.147.vec_ref), custom_call_target="tpu_custom_call" | custom-call | tf_op jit(solution)/shard_map/pallas_call | solution.py:241
  116.1 0.6 fusion.21
  118.0 0.6 copy.20
  118.6 0.6 maximum_multiply_fusion
  119.3 0.7 fusion.11
  (35 shorter events, 0.5 us)
Async XLA Ops:
  0.6 14.6 %copy-start.5 = (s32[256,1]{0,1:T(1,128)S(1)}, s32[256,1]{0,1:T(1,128)}, u32[]{:S(2)}) copy-start(s32[256,1]{0,1:T(1,128)} %param.10) | copy-start | bytes 3076
  0.6 14.9 %copy-start = (bf16[1,256,5000]{1,2,0:T(8,128)(2,1)S(1)}, bf16[1,256,5000]{1,2,0:T(8,128)(2,1)}, u32[]{:S(2)}) copy-start(bf16[1,256,5000]{1,2,0:T(8,128)(2,1)} %param.9) | copy-start | bytes 7680004
  3.3 30.9 %all-to-all-start = ((bf16[128,4,1024]{2,1,0:T(4,128)(2,1)}), bf16[128,4,1024]{2,1,0:T(4,128)(2,1)}, u32[]{:S(2)}, u32[]{:S(2)}) async-start(bf16[128,4,1024]{2,1,0:T(4,128)(2,1)} %bitcast.75), calls=%async_computation | async-start | bytes 2097152 | tf_op jit(solution)/shard_map/all_to_all | solution.py:298
  21.8 5.9 %copy-start.4 = (s32[256]{0:T(256)S(1)}, s32[256]{0:T(256)}, u32[]{:S(2)}) copy-start(s32[256]{0:T(256)} %param.11) | copy-start | bytes 3076
  21.8 6.7 %copy-start.3 = (s32[256]{0:T(256)S(1)}, s32[256]{0:T(256)}, u32[]{:S(2)}) copy-start(s32[256]{0:T(256)} %param.12) | copy-start | bytes 3076
  34.1 18.2 %all-to-all-start.1 = ((bf16[2,128,5000]{1,2,0:T(8,128)(2,1)}), bf16[2,128,5000]{1,2,0:T(8,128)(2,1)}, u32[]{:S(2)}, u32[]{:S(2)}) async-start(bf16[2,128,5000]{1,2,0:T(8,128)(2,1)} %multiply_convert_fusion), calls=%async_computation.1 | async-start | bytes 5120000 | tf_op jit(solution)/shard_map/all_to_all | solution.py:291
  40.3 2.6 %copy-start.2 = (f32[1024]{0:T(1024)S(1)}, f32[1024]{0:T(1024)}, u32[]{:S(2)}) copy-start(f32[1024]{0:T(1024)} %param.17) | copy-start | bytes 12292
  40.3 5.2 %copy-start.1 = (f32[5000]{0:T(1024)S(1)}, f32[5000]{0:T(1024)}, u32[]{:S(2)}) copy-start(f32[5000]{0:T(1024)} %param.16) | copy-start | bytes 60004
  65.1 5.7 %all-to-all-start.2 = ((bf16[2,128,2560]{2,1,0:T(8,128)(2,1)}), bf16[2,128,2560]{2,1,0:T(8,128)(2,1)S(1)}, u32[]{:S(2)}, u32[]{:S(2)}) async-start(bf16[2,128,2560]{2,1,0:T(8,128)(2,1)} %bitcast.16), calls=%async_computation.2 | async-start | bytes 2621440 | tf_op jit(solution)/shard_map/all_to_all | solution.py:312

commit v2 on v1

v2 whole, which is shorter than its diff:
```python
import jax
import jax.numpy as jnp
from jax import lax
from jax.experimental import pallas as pl
from jax.experimental.pallas import tpu as pltpu
from jax.sharding import Mesh
from jax.sharding import PartitionSpec as P

DP = ("dp_0", "dp_1", "dp_2")
TEACH_DP = ("teach", "dp_0", "dp_1", "dp_2")
MESH = pl.DeviceIdType.MESH
F32 = jnp.float32
BF16 = jnp.bfloat16

EPSILON = 1e-05
VOCAB = 5000
WIDTH = 1024
ROWS = 256
STUDENTS = 128

HALF_V = 2560
BLOCK_V = 512
BLOCKS = 5
LAST_WHOLE = 384
TAIL = 4992
THIRDS = ((0, 896), (896, 896), (1792, 768))
WIDEST = 896
STAGE_ROWS = (256, 128, 64, 32, 16, 8)
STAGE_AT = (0, 256, 384, 0, 32, 48)
NARROW = 3
NARROW_ROWS = 448
WIDE_ROWS = 56
PARTS = 6
STAGES = 6
VEC = WIDTH + HALF_V + 128
LOSS_AT = WIDTH + HALF_V
STEP = 16
QUARTERS = 4


def chunk_of(part, row):
    bits = [0] * 6
    for k in range(6):
        bits[(part + k) % 6] = (row >> (5 - k)) & 1
    chip = 0
    for dim in range(3):
        low, high = bits[dim], bits[3 + dim]
        chip = chip * 4 + high * 2 + (high ^ low)
    return chip


def rows_at(k, size=STEP):
    return pl.ds(pl.multiple_of(k * size, size), size)


def lane_ids(rows, width):
    return lax.broadcasted_iota(jnp.int32, (rows, width), 1)


def step_kernel(
    teacher_hbm, weight_hbm, tail_ref, meta_ref, arrived_ref, bias_ref, gain_ref,
    weight_out, gain_out, bias_out, loss_out,
    teacher, soft, soft_in, weight, cols, stats, stats_in, mine_h, their_h,
    normed, scaled, scaled_t, logits, grad,
    lhs, acc, sent, got, sent_wide, got_wide, final, final_in, vec, vec_in,
    teacher_sem, weight_sem, soft_send, soft_recv, pair_send, pair_recv,
    send_sem, recv_sem, vec_send_sem, vec_recv_sem,
):
    t = lax.axis_index("teach")
    place = [lax.axis_index(axis) for axis in DP]

    def partner(bit):
        ids = list(place)
        v = place[bit % 3]
        ids[bit % 3] = (3 - v) if bit >= 3 else (v + 1 - 2 * (v % 2))
        return (t, ids[0], ids[1], ids[2])

    def my_bit(bit):
        v = place[bit % 3]
        return v // 2 if bit >= 3 else (v // 2 + v % 2) % 2

    partners = [partner(bit) for bit in range(6)]
    mine = [my_bit(bit) for bit in range(6)]
    other_core = (1 - t, place[0], place[1], place[2])

    barrier = pltpu.get_barrier_semaphore()
    for device in partners + [other_core]:
        pl.semaphore_signal(barrier, inc=1, device_id=device, device_id_type=MESH)

    size = ROWS // QUARTERS
    teacher_copies = [
        pltpu.make_async_copy(
            teacher_hbm.at[0, q * size:(q + 1) * size, :],
            teacher.at[q * size:(q + 1) * size, :],
            teacher_sem.at[q],
        )
        for q in range(QUARTERS)
    ]
    for copy in teacher_copies:
        copy.start()
    first_column = t * HALF_V
    weight_copies = [
        pltpu.make_async_copy(
            weight_hbm.at[:, pl.ds(pl.multiple_of(first_column + i * BLOCK_V, 128), BLOCK_V)],
            weight.at[:, i * BLOCK_V:(i + 1) * BLOCK_V],
            weight_sem.at[i],
        )
        for i in range(BLOCKS - 1)
    ]
    last_at = (BLOCKS - 1) * BLOCK_V
    last_first = pltpu.make_async_copy(
        weight_hbm.at[:, last_at:HALF_V],
        weight.at[:, last_at:HALF_V],
        weight_sem.at[BLOCKS - 1],
    )
    last_second = pltpu.make_async_copy(
        weight_hbm.at[:, HALF_V + last_at:TAIL],
        weight.at[:, last_at:last_at + LAST_WHOLE],
        weight_sem.at[BLOCKS - 1],
    )
    for copy in weight_copies:
        copy.start()

    @pl.when(t == 0)
    def _():
        last_first.start()

    @pl.when(t == 1)
    def _():
        last_second.start()
        weight[:, last_at + LAST_WHOLE:HALF_V] = tail_ref[...]

    cols[:, 0:8] = jnp.transpose(meta_ref[...])
    routes_col = cols[:, 0:1]
    live = (
        lax.broadcasted_iota(jnp.int32, (ROWS, 1), 0).astype(F32) < cols[:, 3:4]
    ).astype(F32)
    cols[:, 4:5] = live * 0.5
    cols[:, 5:6] = live * 0.5 * cols[:, 1:2]
    frames_here = jnp.sum(live, axis=0, keepdims=True)

    named = (routes_col == lane_ids(ROWS, STUDENTS).astype(F32)).astype(F32)
    earlier = (lane_ids(ROWS, ROWS) < lax.broadcasted_iota(jnp.int32, (ROWS, ROWS), 0)).astype(F32)
    before = jnp.dot(earlier.astype(BF16), named.astype(BF16), preferred_element_type=F32)
    slot = jnp.sum(before * named, axis=1, keepdims=True)
    wanted = routes_col * 4.0 + slot - (t * ROWS).astype(F32)
    pick = (wanted == lane_ids(ROWS, ROWS).astype(F32)).astype(F32).astype(BF16)
    mine_h[...] = jnp.dot(pick, arrived_ref[...], preferred_element_type=F32).astype(BF16)

    def to_pair(source, target, index):
        return pltpu.make_async_remote_copy(
            src_ref=source,
            dst_ref=target,
            send_sem=pair_send.at[index],
            recv_sem=pair_recv.at[index],
            device_id=other_core,
            device_id_type=MESH,
        )

    pl.semaphore_wait(barrier, 7)
    hidden_swap = to_pair(mine_h, their_h, 0)
    hidden_swap.start()

    soft[:, TAIL:2 * HALF_V] = jnp.zeros((ROWS, 2 * HALF_V - TAIL), BF16)
    stat_lane = lane_ids(STEP, 128)

    def soft_step(k, carry):
        rows = rows_at(k)
        x = teacher[rows, :].astype(F32)
        e = jnp.exp(x - jnp.max(x, axis=1, keepdims=True))
        facts = cols[rows, :]
        scale = facts[:, 5:6] / jnp.sum(e, axis=1, keepdims=True)
        hit = lane_ids(STEP, VOCAB) == facts[:, 2:3].astype(jnp.int32)
        s = (e * scale + jnp.where(hit, facts[:, 4:5], 0.0)).astype(BF16)
        soft[rows, 0:VOCAB] = s
        mass = jnp.sum(s.astype(F32), axis=1, keepdims=True)
        stats[rows, :] = jnp.where(stat_lane == 1, mass, 0.0)
        return carry

    away_column = pl.multiple_of((1 - t) * HALF_V, 128)
    own_column = pl.multiple_of(t * HALF_V, 128)
    soft_copies = [
        pltpu.make_async_remote_copy(
            src_ref=soft.at[q * size:(q + 1) * size, pl.ds(away_column, HALF_V)],
            dst_ref=soft_in.at[q * size:(q + 1) * size, :],
            send_sem=soft_send.at[q],
            recv_sem=soft_recv.at[q],
            device_id=other_core,
            device_id_type=MESH,
        )
        for q in range(QUARTERS)
    ]
    for q in range(QUARTERS):
        teacher_copies[q].wait()
        lax.fori_loop(q * size // STEP, (q + 1) * size // STEP, soft_step, 0)
        soft_copies[q].start()

    hidden_swap.wait_recv()
    states = mine_h[...].astype(F32) + their_h[...].astype(F32)
    states = states - jnp.mean(states, axis=1, keepdims=True)
    spread = jnp.mean(jnp.square(states), axis=1, keepdims=True)
    states = states * lax.rsqrt(spread + EPSILON)
    normed[...] = states
    rounded = (states * gain_ref[...]).astype(BF16)
    scaled[...] = rounded
    scaled_t[...] = jnp.transpose(rounded.astype(F32)).reshape(WIDTH // 8, 8, ROWS)

    for i in range(BLOCKS):
        if i < BLOCKS - 1:
            weight_copies[i].wait()
        else:
            @pl.when(t == 0)
            def _():
                last_first.wait()

            @pl.when(t == 1)
            def _():
                last_second.wait()
        at = slice(i * BLOCK_V, (i + 1) * BLOCK_V)
        block = jnp.dot(scaled[...], weight[:, at], preferred_element_type=F32) + bias_ref[t, :, at]
        if i == BLOCKS - 1:
            inside = lane_ids(ROWS, BLOCK_V) < VOCAB - i * BLOCK_V - t * HALF_V
            block = jnp.where(inside, block, -1e30)
        logits[:, at] = block

    for part in range(PARTS):
        half = part // 3
        for row in range(0, 64, 2):
            pair = jnp.concatenate(
                [scaled_t[half * 64 + chunk_of(part, row)], scaled_t[half * 64 + chunk_of(part, row + 1)]],
                axis=0,
            )
            lhs[part, row * 8:row * 8 + 16, :] = pair.astype(BF16)

    def lse_step(k, carry):
        rows = rows_at(k)
        x = logits[rows, :]
        top = jnp.max(x, axis=1, keepdims=True)
        lse = top + jnp.log(jnp.sum(jnp.exp(x - top), axis=1, keepdims=True))
        stats[rows, :] = jnp.where(stat_lane == 0, lse, stats[rows, :])
        return carry

    lax.fori_loop(0, ROWS // STEP, lse_step, 0)
    stats_swap = to_pair(stats, stats_in, 1)
    stats_swap.start()
    for copy in soft_copies:
        copy.wait_recv()
    stats_swap.wait_recv()

    def grad_step(k, loss):
        rows = rows_at(k)
        here, there = stats[rows, :], stats_in[rows, :]
        one, two = here[:, 0:1], there[:, 0:1]
        top = jnp.maximum(one, two)
        lse = top + jnp.log(jnp.exp(one - top) + jnp.exp(two - top))
        mass = here[:, 1:2] + there[:, 1:2]
        log_probs = logits[rows, :] - lse
        both = soft[rows, pl.ds(own_column, HALF_V)].astype(F32) + soft_in[rows, :].astype(F32)
        grad[rows, :] = (mass * jnp.exp(log_probs) - both).astype(BF16)
        return loss - jnp.sum(both * log_probs, axis=1, keepdims=True)

    loss = lax.fori_loop(0, ROWS // STEP, grad_step, jnp.zeros((STEP, 1), F32))

    def copy_of(part, stage):
        width = THIRDS[part % 3][1]
        rows = slice(STAGE_AT[stage], STAGE_AT[stage] + STAGE_ROWS[stage])
        source, target = (sent, got) if stage < NARROW else (sent_wide, got_wide)
        return pltpu.make_async_remote_copy(
            src_ref=source.at[part, rows, 0:width],
            dst_ref=target.at[part, rows, 0:width],
            send_sem=send_sem.at[part * STAGES + stage],
            recv_sem=recv_sem.at[part * STAGES + stage],
            device_id=partners[(part + stage) % 6],
            device_id_type=MESH,
        )

    def vec_copy(stage):
        return pltpu.make_async_remote_copy(
            src_ref=vec.at[stage],
            dst_ref=vec_in.at[stage],
            send_sem=vec_send_sem.at[stage],
            recv_sem=vec_recv_sem.at[stage],
            device_id=partners[stage] if stage < STAGES else other_core,
            device_id_type=MESH,
        )

    for part in (0, 3, 1, 4, 2, 5):
        first, width = THIRDS[part % 3]
        away = pl.multiple_of((1 - mine[part]) * 256, 256)
        block = jnp.dot(
            lhs[part, pl.ds(away, 256), :], grad[:, first:first + width],
            preferred_element_type=F32,
        )
        sent[part, 0:256, 0:width] = block.astype(BF16)
        copy_of(part, 0).start()

    for i in range(4):
        at = slice(i * 256, (i + 1) * 256)
        back = lax.dot_general(
            grad[...], weight[at, :], (((1,), (1,)), ((), ())), preferred_element_type=F32
        )
        vec[0, :, at] = jnp.sum(back * normed[:, at], axis=0, keepdims=True)
    ones = jnp.ones((16, ROWS), BF16)
    vec[0, :, WIDTH:LOSS_AT] = jnp.dot(ones, grad[...], preferred_element_type=F32)[0:1, :]
    lane = lane_ids(1, 128)
    loss_here = jnp.sum(loss, axis=0, keepdims=True)
    vec[0, :, LOSS_AT:VEC] = jnp.where(lane == 0, loss_here, jnp.where(lane == 1, frames_here, 0.0))
    vec_copy(0).start()
    for part in range(PARTS):
        first, width = THIRDS[part % 3]
        stay = pl.multiple_of(mine[part] * 256, 256)
        acc[part, :, 0:width] = jnp.dot(
            lhs[part, pl.ds(stay, 256), :], grad[:, first:first + width],
            preferred_element_type=F32,
        )

    base = [0] * PARTS
    for stage in range(1, STAGES):
        rows = STAGE_ROWS[stage]
        before_at = STAGE_AT[stage - 1]
        arrived = got if stage - 1 < NARROW else got_wide
        for part in (0, 3, 1, 4, 2, 5):
            width = THIRDS[part % 3][1]
            bit = mine[(part + stage) % 6]
            away, stay = (1 - bit) * rows, bit * rows
            unit = min(rows, 16)

            def joined(offset):
                at = pl.multiple_of(base[part] + offset, unit)
                return acc[part, pl.ds(at, rows), 0:width] + arrived[
                    part, pl.ds(pl.multiple_of(before_at + offset, unit), rows), 0:width
                ].astype(F32)

            copy_of(part, stage - 1).wait_recv()
            block = joined(away)
            place_at = slice(STAGE_AT[stage], STAGE_AT[stage] + rows)
            if stage < NARROW:
                sent[part, place_at, 0:width] = block.astype(BF16)
            else:
                sent_wide[part, place_at, 0:width] = block
            copy_of(part, stage).start()
            acc[part, pl.ds(pl.multiple_of(base[part] + stay, unit), rows), 0:width] = joined(stay)
            base[part] = base[part] + stay
        vec_copy(stage - 1).wait_recv()
        vec[stage] = vec[stage - 1] + vec_in[stage - 1]
        vec_copy(stage).start()

    vec_copy(STAGES - 1).wait_recv()
    vec[STAGES] = vec[STAGES - 1] + vec_in[STAGES - 1]
    vec_copy(STAGES).start()
    inverse = 1.0 / vec[STAGES, :, LOSS_AT + 1:LOSS_AT + 2]
    for part in range(PARTS):
        first, width = THIRDS[part % 3]
        copy_of(part, STAGES - 1).wait_recv()
        at = pl.multiple_of(base[part], 8)
        final[part // 3, :, first:first + width] = (
            acc[part, pl.ds(at, 8), 0:width]
            + got_wide[part, STAGE_AT[-1]:STAGE_AT[-1] + 8, 0:width]
        ) * inverse

    swap = to_pair(final.at[1 - t], final_in, 2)
    swap.start()
    vec_copy(STAGES).wait_recv()
    total, beside = vec[STAGES], vec_in[STAGES]
    gain_out[...] = (total[:, 0:WIDTH] + beside[:, 0:WIDTH]) * inverse
    loss_out[...] = (total[:, LOSS_AT:VEC] + beside[:, LOSS_AT:VEC]) * inverse
    rest = VOCAB - HALF_V

    @pl.when(t == 0)
    def _():
        bias_out[:, 0:HALF_V] = total[:, WIDTH:LOSS_AT] * inverse
        bias_out[:, HALF_V:VOCAB] = beside[:, WIDTH:WIDTH + rest] * inverse
        weight_out[:, 0:HALF_V] = final[0]

    @pl.when(t == 1)
    def _():
        bias_out[:, 0:HALF_V] = beside[:, WIDTH:LOSS_AT] * inverse
        bias_out[:, HALF_V:VOCAB] = total[:, WIDTH:WIDTH + rest] * inverse
        weight_out[:, HALF_V:VOCAB] = final[1, :, 0:rest]

    swap.wait_recv()

    @pl.when(t == 0)
    def _():
        weight_out[:, HALF_V:VOCAB] = final_in[:, 0:rest]

    @pl.when(t == 1)
    def _():
        weight_out[:, 0:HALF_V] = final_in[...]

    hidden_swap.wait_send()
    stats_swap.wait_send()
    swap.wait_send()
    for copy in soft_copies:
        copy.wait_send()
    for part in range(PARTS):
        for stage in range(STAGES):
            copy_of(part, stage).wait_send()
    for stage in range(STAGES + 1):
        vec_copy(stage).wait_send()


def distill(teacher_logits, weight, tail, meta, arrived, bias, gain):
    vmem = pl.BlockSpec(memory_space=pltpu.VMEM)
    hbm = pl.BlockSpec(memory_space=pl.ANY)
    dma = pltpu.SemaphoreType.DMA
    return pl.pallas_call(
        step_kernel,
        out_shape=(
            jax.ShapeDtypeStruct((8, VOCAB), F32),
            jax.ShapeDtypeStruct((1, WIDTH), F32),
            jax.ShapeDtypeStruct((1, VOCAB), F32),
            jax.ShapeDtypeStruct((1, 128), F32),
        ),
        in_specs=[hbm, hbm] + [vmem] * 5,
        out_specs=(vmem,) * 4,
        scratch_shapes=[
            pltpu.VMEM((ROWS, VOCAB), BF16),
            pltpu.VMEM((ROWS, 2 * HALF_V), BF16),
            pltpu.VMEM((ROWS, HALF_V), BF16),
            pltpu.VMEM((WIDTH, HALF_V), BF16),
            pltpu.VMEM((ROWS, 128), F32),
            pltpu.VMEM((ROWS, 128), F32),
            pltpu.VMEM((ROWS, 128), F32),
            pltpu.VMEM((ROWS, WIDTH), BF16),
            pltpu.VMEM((ROWS, WIDTH), BF16),
            pltpu.VMEM((ROWS, WIDTH), F32),
            pltpu.VMEM((ROWS, WIDTH), BF16),
            pltpu.VMEM((WIDTH // 8, 8, ROWS), F32),
            pltpu.VMEM((ROWS, HALF_V), F32),
            pltpu.VMEM((ROWS, HALF_V), BF16),
            pltpu.VMEM((PARTS, 512, ROWS), BF16),
            pltpu.VMEM((PARTS, 256, WIDEST), F32),
            pltpu.VMEM((PARTS, NARROW_ROWS, WIDEST), BF16),
            pltpu.VMEM((PARTS, NARROW_ROWS, WIDEST), BF16),
            pltpu.VMEM((PARTS, WIDE_ROWS, WIDEST), F32),
            pltpu.VMEM((PARTS, WIDE_ROWS, WIDEST), F32),
            pltpu.VMEM((2, 8, HALF_V), F32),
            pltpu.VMEM((8, HALF_V), F32),
            pltpu.VMEM((STAGES + 1, 1, VEC), F32),
            pltpu.VMEM((STAGES + 1, 1, VEC), F32),
            dma((QUARTERS,)),
            dma((BLOCKS,)),
            dma((QUARTERS,)),
            dma((QUARTERS,)),
            dma((3,)),
            dma((3,)),
            dma((PARTS * STAGES,)),
            dma((PARTS * STAGES,)),
            dma((STAGES + 1,)),
            dma((STAGES + 1,)),
        ],
        compiler_params=pltpu.CompilerParams(
            collective_id=0, has_side_effects=True, vmem_limit_bytes=60 * 1024 * 1024
        ),
    )(teacher_logits, weight, tail, meta, arrived, bias, gain)


def body(
    teacher_logits, routes, agreement, targets, lengths, student_hidden, out_weight, out_bias, gain
):
    arrived = lax.all_to_all(student_hidden, DP, split_axis=0, concat_axis=0, tiled=True)
    meta = jnp.concatenate(
        [
            routes.reshape(1, ROWS),
            agreement[None],
            targets[None],
            jnp.broadcast_to(lengths[:, None], (1, ROWS)),
            jnp.zeros((4, ROWS), jnp.int32),
        ]
    ).astype(F32)
    tail = jnp.pad(out_weight[:, TAIL:], ((0, 0), (0, 2 * HALF_V - VOCAB)))
    bias = jnp.pad(out_bias, (0, 2 * HALF_V - VOCAB)).reshape(2, 1, HALF_V)
    weight_grad, gain_grad, bias_grad, loss = distill(
        teacher_logits, out_weight, tail, meta, arrived, bias, gain[None]
    )
    return (weight_grad, gain_grad[0], bias_grad[0], loss[0, 0])


def solution(mesh):
    finer = Mesh(
        mesh.devices.reshape(mesh.shape["teach"], 4, 4, 4), ("teach", "dp_0", "dp_1", "dp_2")
    )
    in_specs = (
        P("teach", DP, None),
        P(DP, None),
        P(DP),
        P(DP),
        P(DP),
        P(TEACH_DP, None),
        P(),
        P(),
        P(),
    )
    out_specs = (P(TEACH_DP, None), P(), P(), P())
    return jax.shard_map(body, mesh=finer, in_specs=in_specs, out_specs=out_specs, check_vma=False)
```

time: 122 us -> 111 us (0.910)
  Pallas kernels: 41.5 us -> 66 us
  other arithmetic: 17.4 us -> 0.6 us
  matrix products: 12.1 us -> 0 us
  starting transfers between devices: 21.8 us -> 12 us
  local copies, waits for them, and re-layouts: 19.9 us -> 28.5 us
  blocking collectives: 2.36 us -> 0 us
  between operations: 4.64 us -> 3.08 us
  waiting for transfers between devices: 1.29 us -> 0.01 us
    pallas_call x1, Pallas kernels: 41.5 us -> 66 us  [distill(): pl.pallas_call(step_kernel, out_shape=(jax.ShapeDtypeStruct((8, VOCAB), F...]
    unnamed x15 -> x7, local copies, waits for them, and re-layouts: 0.66 us -> 22.4 us
    dot_general x3 -> x0, matrix products: 12.1 us -> none  [the longest x1 6.12 us: student_forward(): jnp.dot(scaled, out_weight, preferred_element_type=jnp.float32)]
    convert_element_type x2 -> x0, local copies, waits for them, and re-layouts: 9.89 us -> none  [soft_targets(): probs_teacher = jax.nn.softmax(teacher_rows.astype(jnp.float32), axis=-1)]
    all_to_all x3 -> x1, starting transfers between devices: 21.8 us -> 12 us  [body(): lax.all_to_all(student_hidden, DP, split_axis=0, concat_axis=0, tiled=True)]
    convert_element_type x6 -> x1, other arithmetic: 8.43 us -> 0.6 us  [body(): meta = jnp.concatenate([routes.reshape(1, ROWS), agreement[None], targets...]
    reduce_sum x7 -> x0, other arithmetic: 5.79 us -> none  [the longest x1 2.96 us: body(): jnp.sum((both_soft[0].astype(jnp.float32) + both_soft[1].astype(jnp.float...]
    all_to_all x0 -> x2, local copies, waits for them, and re-layouts: none -> 3.03 us  [body(): lax.all_to_all(student_hidden, DP, split_axis=0, concat_axis=0, tiled=True)]
  transfers between devices with their start and end apart: 3 -> 1, of which waited for: 1 -> 0; matrix products, arithmetic and copies ran while one was open for 23% -> 20% of each run, Pallas kernels for 0% -> 0%
where the time goes in v2:
time: 111 us; the launch traced here: 110 us
  Pallas kernels  66 us (59%)
  local copies, waits for them, and re-layouts  28.5 us (26%)
  starting transfers between devices  12 us (11%)
  between operations  3.08 us (3%)
    pallas_call x1, Pallas kernels, distill(): pl.pallas_call(step_kernel, out_shape=(jax.ShapeDtypeStruct((8, VOCAB), F...  66 us
    unnamed x7, local copies, waits for them, and re-layouts  22.4 us
    all_to_all x1, starting transfers between devices, body(): lax.all_to_all(student_hidden, DP, split_axis=0, concat_axis=0, tiled=True)  12 us
    all_to_all x2, local copies, waits for them, and re-layouts, body(): lax.all_to_all(student_hidden, DP, split_axis=0, concat_axis=0, tiled=True)  3.03 us
  transfers between devices with their start and end apart: 1, of which 0 were waited for; matrix products, arithmetic and copies ran while one was open for 20% of the time, Pallas kernels for 0%

profile of v2, /device:TPU:1, one launch (start us, length us, event | category | flops | bytes accessed | tf_op | source)
XLA Modules:
  0.0 110.1 jit_solution(14667205800205080676)
XLA Ops:
  0.6 2.1 %all_to_all.7 = bf16[64,4,1024]{2,1,0:T(4,128)(2,1)} reshape(bf16[256,1024]{1,0:T(8,128)(2,1)} %param.14) | data formatting | bytes 1048576 | tf_op jit(solution)/shard_map/all_to_all | solution.py:462
  2.7 12.0 %all-to-all-start = ((bf16[64,4,1024]{2,1,0:T(4,128)(2,1)}), bf16[64,4,1024]{2,1,0:T(4,128)(2,1)S(1)}, u32[]{:S(2)}, u32[]{:S(2)}) async-start(bf16[64,4,1024]{2,1,0:T(4,128)(2,1)} %all_to_all.7), calls=%async_computation | async-start | bytes 1048576 | tf_op jit(solution)/shard_map/all_to_all | solution.py:462
  15.3 0.7 concatenate.3
  16.1 0.6 convert_element_type.7.meta_ref
  16.7 4.5 %copy.14.teacher_hbm = bf16[1,256,5000]{2,1,0:T(8,128)(2,1)} copy(bf16[1,256,5000]{1,2,0:T(8,128)(2,1)} %param.9) | data formatting | bytes 5120000 | tf_op args[0]
  21.2 0.0 copy-start
  21.2 13.7 %copy.15.weight_hbm = bf16[1024,5000]{1,0:T(8,128)(2,1)} copy(bf16[1024,5000]{0,1:T(8,128)(2,1)} %param.15) | data formatting | bytes 20480000 | tf_op args[6]
  34.9 1.0 slice.8
  35.8 0.0 copy-done
  35.9 0.6 pad.9
  36.5 0.8 pad.8.tail_ref
  37.2 0.0 all-to-all-done
  37.2 1.0 all_to_all.9.arrived_ref
  38.2 66.0 %shard_map.120 = (f32[8,5000]{1,0:T(8,128)}, f32[1,1024]{1,0:T(1,128)}, f32[1,5000]{1,0:T(1,128)}, f32[1,128]{1,0:T(1,128)}) custom-call(bf16[1,256,5000]{2,1,0:T(8,128)(2,1)} %copy.14.teacher_hbm, bf16[1024,5000]{1,0:T(8,128)(2,1)} %copy.15.weight_hbm, bf16[1024,128]{1,0:T(8,128)(2,1)} %pad.8.tail_ref, f32[8,256]{1,0:T(8,128)} %convert_element_type.7.meta_ref, ...), custom_call_target="tpu_custom_call" | custom-call | tf_op jit(solution)/shard_map/pallas_call | solution.py:407
  104.2 1.6 %copy.21 = f32[8,5000]{1,0:T(8,128)} copy(f32[8,5000]{1,0:T(8,128)} %get-tuple-element.16) | data formatting | bytes 320000
  105.8 1.3 %copy.22 = f32[1024]{0:T(1024)} copy(f32[1024]{0:T(1024)} %bitcast.14) | data formatting | bytes 8192
  107.1 1.3 %copy.23 = f32[5000]{0:T(1024)} copy(f32[5000]{0:T(1024)} %bitcast.12) | data formatting | bytes 40000
  (2 shorter events, 0.0 us)
Async XLA Ops:
  2.7 34.5 %all-to-all-start = ((bf16[64,4,1024]{2,1,0:T(4,128)(2,1)}), bf16[64,4,1024]{2,1,0:T(4,128)(2,1)S(1)}, u32[]{:S(2)}, u32[]{:S(2)}) async-start(bf16[64,4,1024]{2,1,0:T(4,128)(2,1)} %all_to_all.7), calls=%async_computation | async-start | bytes 1048576 | tf_op jit(solution)/shard_map/all_to_all | solution.py:462
  21.2 14.7 %copy-start = (f32[5000]{0:T(1024)S(1)}, f32[5000]{0:T(1024)}, u32[]{:S(2)}) copy-start(f32[5000]{0:T(1024)} %param.16) | copy-start | bytes 60004

commit v3 on v2

v3 whole, which is shorter than its diff:
```python
import jax
import jax.numpy as jnp
from jax import lax
from jax.experimental import pallas as pl
from jax.experimental.pallas import tpu as pltpu
from jax.sharding import Mesh
from jax.sharding import PartitionSpec as P

DP = ("dp_0", "dp_1", "dp_2")
TEACH_DP = ("teach", "dp_0", "dp_1", "dp_2")
MESH = pl.DeviceIdType.MESH
F32 = jnp.float32
BF16 = jnp.bfloat16

EPSILON = 1e-05
VOCAB = 5000
WIDTH = 1024
ROWS = 256
STUDENTS = 128

HALF_V = 2560
BLOCK_V = 512
BLOCKS = 5
THIRDS = ((0, 896), (896, 896), (1792, 768))
WIDEST = 896
STAGE_ROWS = (256, 128, 64, 32, 16, 8)
STAGE_AT = (0, 256, 384, 0, 32, 48)
NARROW = 3
NARROW_ROWS = 448
WIDE_ROWS = 56
PARTS = 6
STAGES = 6
VEC = WIDTH + HALF_V + 128
LOSS_AT = WIDTH + HALF_V
STEP = 64
PIECES = 4
CHIPS = 64


def chunk_of(part, row):
    bits = [0] * 6
    for k in range(6):
        bits[(part + k) % 6] = (row >> (5 - k)) & 1
    chip = 0
    for dim in range(3):
        low, high = bits[dim], bits[3 + dim]
        chip = chip * 4 + high * 2 + (high ^ low)
    return chip


def rows_at(k, size=STEP):
    return pl.ds(pl.multiple_of(k * size, size), size)


def lane_ids(rows, width):
    return lax.broadcasted_iota(jnp.int32, (rows, width), 1)


def sublane_ids(rows, width):
    return lax.broadcasted_iota(jnp.int32, (rows, width), 0)


def folded(x, rows, op):
    groups = x.reshape(x.shape[0] // rows, rows, x.shape[1])
    total = groups[0]
    for k in range(1, groups.shape[0]):
        total = op(total, groups[k])
    return total


def step_kernel(
    teacher_hbm, weight_hbm, hidden_ref, routes_ref, agree_ref, target_ref, length_ref, bias_ref, gain_ref,
    weight_out, gain_out, bias_out, loss_out,
    teacher, soft, soft_in, weight, message, arrived, stats, stats_in, mine_h, their_h,
    bias_row, bias_t, normed, scaled, scaled_t, logits, grad, grad_n,
    lhs, acc, sent, got, sent_wide, got_wide, final, final_in, vec, vec_in,
    teacher_sem, weight_sem, hidden_send, hidden_recv, soft_send, soft_recv, pair_send, pair_recv,
    send_sem, recv_sem, vec_send_sem, vec_recv_sem,
):
    t = lax.axis_index("teach")
    place = [lax.axis_index(axis) for axis in DP]
    me = place[0] * 16 + place[1] * 4 + place[2]

    def partner(bit):
        ids = list(place)
        v = place[bit % 3]
        ids[bit % 3] = (3 - v) if bit >= 3 else (v + 1 - 2 * (v % 2))
        return (t, ids[0], ids[1], ids[2])

    def my_bit(bit):
        v = place[bit % 3]
        return v // 2 if bit >= 3 else (v // 2 + v % 2) % 2

    partners = [partner(bit) for bit in range(6)]
    mine = [my_bit(bit) for bit in range(6)]
    other_core = (1 - t, place[0], place[1], place[2])

    def moved(k, sign):
        step = (k * 21) % CHIPS
        steps = (step // 16, (step // 4) % 4, step % 4)
        return [(v + 4 + sign * s) % 4 for v, s in zip(place, steps)]

    def index_of(ids):
        return ids[0] * 16 + ids[1] * 4 + ids[2]

    barrier = pltpu.get_barrier_semaphore()
    pl.semaphore_signal(barrier, inc=1, device_id=other_core, device_id_type=MESH)

    def greet(k, carry):
        ids = moved(k, 1)
        pl.semaphore_signal(
            barrier, inc=1, device_id=(t, ids[0], ids[1], ids[2]), device_id_type=MESH
        )
        return carry

    lax.fori_loop(1, CHIPS, greet, 0)

    cuts = (0, 1280, 2560, 3840, VOCAB)
    teacher_copies = [
        pltpu.make_async_copy(
            teacher_hbm.at[cuts[q]:cuts[q + 1], :],
            teacher.at[cuts[q]:cuts[q + 1], :],
            teacher_sem.at[q],
        )
        for q in range(PIECES)
    ]
    for copy in teacher_copies:
        copy.start()
    weight_copies = [
        pltpu.make_async_copy(
            weight_hbm.at[pl.ds(pl.multiple_of(t * HALF_V + i * BLOCK_V, BLOCK_V), BLOCK_V), :],
            weight.at[i * BLOCK_V:(i + 1) * BLOCK_V, :],
            weight_sem.at[i],
        )
        for i in range(BLOCKS - 1)
    ]
    last_at = (BLOCKS - 1) * BLOCK_V
    rest = VOCAB - HALF_V
    last_first = pltpu.make_async_copy(
        weight_hbm.at[last_at:HALF_V, :],
        weight.at[last_at:HALF_V, :],
        weight_sem.at[BLOCKS - 1],
    )
    last_second = pltpu.make_async_copy(
        weight_hbm.at[HALF_V + last_at:VOCAB, :],
        weight.at[last_at:rest, :],
        weight_sem.at[BLOCKS - 1],
    )
    for copy in weight_copies:
        copy.start()

    @pl.when(t == 0)
    def _():
        last_first.start()

    @pl.when(t == 1)
    def _():
        last_second.start()
        weight[rest:HALF_V, :] = jnp.zeros((HALF_V - rest, WIDTH), BF16)

    low = sublane_ids(8, 512) < 4

    def pack(k, carry):
        x = hidden_ref[pl.ds(pl.multiple_of(k * 16, 16), 16), :].astype(F32)
        for i in range(2):
            left, right = x[8 * i:8 * i + 8, 0:512], x[8 * i:8 * i + 8, 512:1024]
            message[4 * k + 2 * i] = jnp.where(low, left, pltpu.roll(right, 4, 0)).astype(BF16)
            message[4 * k + 2 * i + 1] = jnp.where(low, pltpu.roll(left, 4, 0), right).astype(BF16)
        return carry

    lax.fori_loop(0, ROWS // 16, pack, 0)
    arrived[me] = message[me]

    routes_row = routes_ref[...].astype(F32)
    live = (lane_ids(1, ROWS) < length_ref[...]).astype(F32)
    half_live = live * 0.5
    weight_row = half_live * agree_ref[...].astype(F32)
    frames_here = jnp.sum(live, axis=1, keepdims=True)
    named = (routes_row == sublane_ids(STUDENTS, ROWS).astype(F32)).astype(F32)
    earlier = (sublane_ids(ROWS, ROWS) < lane_ids(ROWS, ROWS)).astype(F32)
    before = jnp.dot(named.astype(BF16), earlier.astype(BF16), preferred_element_type=F32)
    slot = jnp.sum(before * named, axis=0, keepdims=True)
    wanted = (routes_row - (t * CHIPS).astype(F32)) * 8.0 + slot
    wanted = jnp.transpose(jnp.broadcast_to(wanted, (8, ROWS)))[:, 0:1]

    teacher[VOCAB:2 * HALF_V, :] = jnp.full((2 * HALF_V - VOCAB, ROWS), -1e30, BF16)

    def max_step(k, top):
        return jnp.maximum(top, folded(teacher[rows_at(k), :], 16, jnp.maximum))

    top = jnp.full((16, ROWS), -1e30, BF16)
    for q in range(PIECES):
        teacher_copies[q].wait()
        last = cuts[q + 1] // STEP if q < PIECES - 1 else 2 * HALF_V // STEP
        top = lax.fori_loop(cuts[q] // STEP, last, max_step, top, unroll=2)
    top = jnp.max(top.astype(F32), axis=0, keepdims=True)

    def sum_step(k, total):
        return total + folded(jnp.exp(teacher[rows_at(k), :].astype(F32) - top), 8, jnp.add)

    total = lax.fori_loop(0, 2 * HALF_V // STEP, sum_step, jnp.zeros((8, ROWS), F32), unroll=2)
    scale_row = weight_row / jnp.sum(total, axis=0, keepdims=True)

    pl.semaphore_wait(barrier, CHIPS)

    def hidden_copy(k, receiving):
        ids = moved(k, 1)
        source = index_of(moved(k, -1)) if receiving else me
        return pltpu.make_async_remote_copy(
            src_ref=message.at[index_of(ids)],
            dst_ref=arrived.at[source],
            send_sem=hidden_send.at[k],
            recv_sem=hidden_recv.at[k],
            device_id=(t, ids[0], ids[1], ids[2]),
            device_id_type=MESH,
        )

    def send_hidden(k, carry):
        hidden_copy(k, False).start()
        return carry

    lax.fori_loop(1, CHIPS, send_hidden, 0)

    target_row = target_ref[...]
    step_rows = sublane_ids(STEP, ROWS)

    def soft_step(k, mass):
        rows = rows_at(k)
        e = jnp.exp(teacher[rows, :].astype(F32) - top)
        hit = step_rows == target_row - k * STEP
        s = (e * scale_row + jnp.where(hit, half_live, 0.0)).astype(BF16)
        soft[rows, :] = s
        return mass + folded(s.astype(F32), 8, jnp.add)

    piece = HALF_V // PIECES
    soft_copies = [
        pltpu.make_async_remote_copy(
            src_ref=soft.at[pl.ds(pl.multiple_of((1 - t) * HALF_V + q * piece, 64), piece), :],
            dst_ref=soft_in.at[q * piece:(q + 1) * piece, :],
            send_sem=soft_send.at[q],
            recv_sem=soft_recv.at[q],
            device_id=other_core,
            device_id_type=MESH,
        )
        for q in range(PIECES)
    ]
    mass = jnp.zeros((8, ROWS), F32)
    for q in range(PIECES):
        first = (1 - t) * (HALF_V // STEP) + q * (piece // STEP)
        mass = lax.fori_loop(first, first + piece // STEP, soft_step, mass)
        soft_copies[q].start()
    first = t * (HALF_V // STEP)
    mass = lax.fori_loop(first, first + HALF_V // STEP, soft_step, mass)
    mass = jnp.sum(mass, axis=0, keepdims=True)

    bias_row[:, 0:VOCAB] = bias_ref[...]
    bias_row[:, VOCAB:2 * HALF_V] = jnp.zeros((1, 2 * HALF_V - VOCAB), F32)

    def bias_step(k, carry):
        strip = bias_row[:, pl.ds(pl.multiple_of(t * HALF_V + k * 128, 128), 128)]
        bias_t[rows_at(k, 128), :] = jnp.transpose(jnp.broadcast_to(strip, (128, 128)))
        return carry

    lax.fori_loop(0, HALF_V // 128, bias_step, 0)

    def wait_hidden(k, carry):
        hidden_copy(k, True).wait_recv()
        return carry

    lax.fori_loop(1, CHIPS, wait_hidden, 0)
    rows_in = arrived[...].reshape(CHIPS * 8, 512)
    for i in range(2):
        pick = (wanted + 4.0 * i == lane_ids(ROWS, CHIPS * 8).astype(F32)).astype(F32).astype(BF16)
        mine_h[:, 512 * i:512 * i + 512] = jnp.dot(
            pick, rows_in, preferred_element_type=F32
        ).astype(BF16)

    def to_pair(source, target, index):
        return pltpu.make_async_remote_copy(
            src_ref=source,
            dst_ref=target,
            send_sem=pair_send.at[index],
            recv_sem=pair_recv.at[index],
            device_id=other_core,
            device_id_type=MESH,
        )

    hidden_swap = to_pair(mine_h, their_h, 0)
    hidden_swap.start()

    hidden_swap.wait_recv()
    states = mine_h[...].astype(F32) + their_h[...].astype(F32)
    states = states - jnp.mean(states, axis=1, keepdims=True)
    spread = jnp.mean(jnp.square(states), axis=1, keepdims=True)
    states = states * lax.rsqrt(spread + EPSILON)
    normed[...] = states
    turned = jnp.transpose((states * gain_ref[...]).astype(BF16).astype(F32))
    scaled_t[...] = turned.reshape(WIDTH // 8, 8, ROWS)
    scaled[...] = turned.astype(BF16)

    peak = jnp.full((8, ROWS), -1e30, F32)
    for i in range(BLOCKS):
        if i < BLOCKS - 1:
            weight_copies[i].wait()
        else:
            @pl.when(t == 0)
            def _():
                last_first.wait()

            @pl.when(t == 1)
            def _():
                last_second.wait()
        at = slice(i * BLOCK_V, (i + 1) * BLOCK_V)
        slope = bias_t[at, :]
        block = jnp.dot(weight[at, :], scaled[...], preferred_element_type=F32)
        block = block + jnp.concatenate([slope, slope], axis=1)
        if i == BLOCKS - 1:
            inside = sublane_ids(BLOCK_V, ROWS) < VOCAB - i * BLOCK_V - t * HALF_V
            block = jnp.where(inside, block, -1e30)
        logits[at, :] = block
        peak = jnp.maximum(peak, folded(block, 8, jnp.maximum))
    peak = jnp.max(peak, axis=0, keepdims=True)

    def lse_step(k, total):
        return total + folded(jnp.exp(logits[rows_at(k), :] - peak), 8, jnp.add)

    total = lax.fori_loop(0, HALF_V // STEP, lse_step, jnp.zeros((8, ROWS), F32), unroll=2)
    lse = peak + jnp.log(jnp.sum(total, axis=0, keepdims=True))
    stats[...] = jnp.concatenate([lse, mass, jnp.zeros((6, ROWS), F32)], axis=0)
    stats_swap = to_pair(stats, stats_in, 1)
    stats_swap.start()

    for part in range(PARTS):
        half = part // 3
        for row in range(0, 64, 2):
            pair = jnp.concatenate(
                [scaled_t[half * 64 + chunk_of(part, row)], scaled_t[half * 64 + chunk_of(part, row + 1)]],
                axis=0,
            )
            lhs[part, row * 8:row * 8 + 16, :] = pair.astype(BF16)

    for copy in soft_copies:
        copy.wait_recv()
    stats_swap.wait_recv()
    there = stats_in[...]
    other_lse = there[0:1, :]
    highest = jnp.maximum(lse, other_lse)
    lse = highest + jnp.log(jnp.exp(lse - highest) + jnp.exp(other_lse - highest))
    mass = mass + there[1:2, :]

    def grad_step(k, loss):
        rows = rows_at(k)
        log_probs = logits[rows, :] - lse
        own = pl.ds(pl.multiple_of(t * HALF_V + k * STEP, STEP), STEP)
        both = soft[own, :].astype(F32) + soft_in[rows, :].astype(F32)
        grad[rows, :] = (mass * jnp.exp(log_probs) - both).astype(BF16)
        return loss - folded(both * log_probs, 8, jnp.add)

    def copy_of(part, stage):
        width = THIRDS[part % 3][1]
        rows = slice(STAGE_AT[stage], STAGE_AT[stage] + STAGE_ROWS[stage])
        source, target = (sent, got) if stage < NARROW else (sent_wide, got_wide)
        return pltpu.make_async_remote_copy(
            src_ref=source.at[part, rows, 0:width],
            dst_ref=target.at[part, rows, 0:width],
            send_sem=send_sem.at[part * STAGES + stage],
            recv_sem=recv_sem.at[part * STAGES + stage],
            device_id=partners[(part + stage) % 6],
            device_id_type=MESH,
        )

    def vec_copy(stage):
        return pltpu.make_async_remote_copy(
            src_ref=vec.at[stage],
            dst_ref=vec_in.at[stage],
            send_sem=vec_send_sem.at[stage],
            recv_sem=vec_recv_sem.at[stage],
            device_id=partners[stage] if stage < STAGES else other_core,
            device_id_type=MESH,
        )

    def product(part, at):
        first, width = THIRDS[part % 3]
        return lax.dot_general(
            lhs[part, pl.ds(pl.multiple_of(at, 256), 256), :], grad[first:first + width, :],
            (((1,), (1,)), ((), ())), preferred_element_type=F32,
        )

    loss = jnp.zeros((8, ROWS), F32)
    for third in range(3):
        first, width = THIRDS[third]
        loss = lax.fori_loop(first // STEP, (first + width) // STEP, grad_step, loss)
        for part in (third, third + 3):
            sent[part, 0:256, 0:width] = product(part, (1 - mine[part]) * 256).astype(BF16)
            copy_of(part, 0).start()

    for part in range(PARTS):
        acc[part, :, 0:THIRDS[part % 3][1]] = product(part, mine[part] * 256)
    for i in range(BLOCKS):
        at = slice(i * BLOCK_V, (i + 1) * BLOCK_V)
        grad_n[:, at] = jnp.transpose(grad[at, :].astype(F32)).astype(BF16)
    for i in range(4):
        at = slice(i * 256, (i + 1) * 256)
        back = jnp.dot(grad_n[...], weight[:, at], preferred_element_type=F32)
        vec[0, :, at] = jnp.sum(back * normed[:, at], axis=0, keepdims=True)
    ones = jnp.ones((16, ROWS), BF16)
    vec[0, :, WIDTH:LOSS_AT] = jnp.dot(ones, grad_n[...], preferred_element_type=F32)[0:1, :]
    lane = lane_ids(1, 128)
    loss_here = jnp.sum(jnp.sum(loss, axis=0, keepdims=True), axis=1, keepdims=True)
    vec[0, :, LOSS_AT:VEC] = jnp.where(lane == 0, loss_here, jnp.where(lane == 1, frames_here, 0.0))
    vec_copy(0).start()

    base = [0] * PARTS
    for stage in range(1, STAGES):
        rows = STAGE_ROWS[stage]
        before_at = STAGE_AT[stage - 1]
        incoming = got if stage - 1 < NARROW else got_wide
        for part in (0, 3, 1, 4, 2, 5):
            width = THIRDS[part % 3][1]
            bit = mine[(part + stage) % 6]
            away, stay = (1 - bit) * rows, bit * rows
            unit = min(rows, 16)

            def joined(offset):
                at = pl.multiple_of(base[part] + offset, unit)
                return acc[part, pl.ds(at, rows), 0:width] + incoming[
                    part, pl.ds(pl.multiple_of(before_at + offset, unit), rows), 0:width
                ].astype(F32)

            copy_of(part, stage - 1).wait_recv()
            block = joined(away)
            place_at = slice(STAGE_AT[stage], STAGE_AT[stage] + rows)
            if stage < NARROW:
                sent[part, place_at, 0:width] = block.astype(BF16)
            else:
                sent_wide[part, place_at, 0:width] = block
            copy_of(part, stage).start()
            acc[part, pl.ds(pl.multiple_of(base[part] + stay, unit), rows), 0:width] = joined(stay)
            base[part] = base[part] + stay
        vec_copy(stage - 1).wait_recv()
        vec[stage] = vec[stage - 1] + vec_in[stage - 1]
        vec_copy(stage).start()

    vec_copy(STAGES - 1).wait_recv()
    vec[STAGES] = vec[STAGES - 1] + vec_in[STAGES - 1]
    vec_copy(STAGES).start()
    inverse = 1.0 / vec[STAGES, :, LOSS_AT + 1:LOSS_AT + 2]
    for part in range(PARTS):
        first, width = THIRDS[part % 3]
        copy_of(part, STAGES - 1).wait_recv()
        at = pl.multiple_of(base[part], 8)
        final[part // 3, :, first:first + width] = (
            acc[part, pl.ds(at, 8), 0:width]
            + got_wide[part, STAGE_AT[-1]:STAGE_AT[-1] + 8, 0:width]
        ) * inverse

    swap = to_pair(final.at[1 - t], final_in, 2)
    swap.start()
    vec_copy(STAGES).wait_recv()
    total, beside = vec[STAGES], vec_in[STAGES]
    gain_out[...] = (total[:, 0:WIDTH] + beside[:, 0:WIDTH]) * inverse
    loss_out[...] = (total[:, LOSS_AT:VEC] + beside[:, LOSS_AT:VEC]) * inverse

    @pl.when(t == 0)
    def _():
        bias_out[:, 0:HALF_V] = total[:, WIDTH:LOSS_AT] * inverse
        bias_out[:, HALF_V:VOCAB] = beside[:, WIDTH:WIDTH + rest] * inverse
        weight_out[:, 0:HALF_V] = final[0]

    @pl.when(t == 1)
    def _():
        bias_out[:, 0:HALF_V] = beside[:, WIDTH:LOSS_AT] * inverse
        bias_out[:, HALF_V:VOCAB] = total[:, WIDTH:WIDTH + rest] * inverse
        weight_out[:, HALF_V:VOCAB] = final[1, :, 0:rest]

    swap.wait_recv()

    @pl.when(t == 0)
    def _():
        weight_out[:, HALF_V:VOCAB] = final_in[:, 0:rest]

    @pl.when(t == 1)
    def _():
        weight_out[:, 0:HALF_V] = final_in[...]

    def sent_hidden(k, carry):
        hidden_copy(k, False).wait_send()
        return carry

    lax.fori_loop(1, CHIPS, sent_hidden, 0)
    hidden_swap.wait_send()
    stats_swap.wait_send()
    swap.wait_send()
    for copy in soft_copies:
        copy.wait_send()
    for part in range(PARTS):
        for stage in range(STAGES):
            copy_of(part, stage).wait_send()
    for stage in range(STAGES + 1):
        vec_copy(stage).wait_send()


def distill(teacher, weight, *small):
    vmem = pl.BlockSpec(memory_space=pltpu.VMEM)
    hbm = pl.BlockSpec(memory_space=pl.ANY)
    dma = pltpu.SemaphoreType.DMA
    return pl.pallas_call(
        step_kernel,
        out_shape=(
            jax.ShapeDtypeStruct((8, VOCAB), F32),
            jax.ShapeDtypeStruct((1, WIDTH), F32),
            jax.ShapeDtypeStruct((1, VOCAB), F32),
            jax.ShapeDtypeStruct((1, 128), F32),
        ),
        in_specs=[hbm, hbm] + [vmem] * len(small),
        out_specs=(vmem,) * 4,
        scratch_shapes=[
            pltpu.VMEM((2 * HALF_V, ROWS), BF16),
            pltpu.VMEM((2 * HALF_V, ROWS), BF16),
            pltpu.VMEM((HALF_V, ROWS), BF16),
            pltpu.VMEM((HALF_V, WIDTH), BF16),
            pltpu.VMEM((CHIPS, 8, 512), BF16),
            pltpu.VMEM((CHIPS, 8, 512), BF16),
            pltpu.VMEM((8, ROWS), F32),
            pltpu.VMEM((8, ROWS), F32),
            pltpu.VMEM((ROWS, WIDTH), BF16),
            pltpu.VMEM((ROWS, WIDTH), BF16),
            pltpu.VMEM((1, 2 * HALF_V), F32),
            pltpu.VMEM((HALF_V, 128), F32),
            pltpu.VMEM((ROWS, WIDTH), F32),
            pltpu.VMEM((WIDTH, ROWS), BF16),
            pltpu.VMEM((WIDTH // 8, 8, ROWS), F32),
            pltpu.VMEM((HALF_V, ROWS), F32),
            pltpu.VMEM((HALF_V, ROWS), BF16),
            pltpu.VMEM((ROWS, HALF_V), BF16),
            pltpu.VMEM((PARTS, 512, ROWS), BF16),
            pltpu.VMEM((PARTS, 256, WIDEST), F32),
            pltpu.VMEM((PARTS, NARROW_ROWS, WIDEST), BF16),
            pltpu.VMEM((PARTS, NARROW_ROWS, WIDEST), BF16),
            pltpu.VMEM((PARTS, WIDE_ROWS, WIDEST), F32),
            pltpu.VMEM((PARTS, WIDE_ROWS, WIDEST), F32),
            pltpu.VMEM((2, 8, HALF_V), F32),
            pltpu.VMEM((8, HALF_V), F32),
            pltpu.VMEM((STAGES + 1, 1, VEC), F32),
            pltpu.VMEM((STAGES + 1, 1, VEC), F32),
            dma((PIECES,)),
            dma((BLOCKS,)),
            dma((CHIPS,)),
            dma((CHIPS,)),
            dma((PIECES,)),
            dma((PIECES,)),
            dma((3,)),
            dma((3,)),
            dma((PARTS * STAGES,)),
            dma((PARTS * STAGES,)),
            dma((STAGES + 1,)),
            dma((STAGES + 1,)),
        ],
        compiler_params=pltpu.CompilerParams(
            collective_id=0, has_side_effects=True, vmem_limit_bytes=60 * 1024 * 1024
        ),
    )(teacher, weight, *small)


def body(
    teacher_logits, routes, agreement, targets, lengths, student_hidden, out_weight, out_bias, gain
):
    weight_grad, gain_grad, bias_grad, loss = distill(
        teacher_logits[0].T,
        out_weight.T,
        student_hidden,
        routes.reshape(1, ROWS),
        agreement[None],
        targets[None],
        lengths[None],
        out_bias[None],
        gain[None],
    )
    return (weight_grad, gain_grad[0], bias_grad[0], loss[0, 0])


def solution(mesh):
    finer = Mesh(
        mesh.devices.reshape(mesh.shape["teach"], 4, 4, 4), ("teach", "dp_0", "dp_1", "dp_2")
    )
    in_specs = (
        P("teach", DP, None),
        P(DP, None),
        P(DP),
        P(DP),
        P(DP),
        P(TEACH_DP, None),
        P(),
        P(),
        P(),
    )
    out_specs = (P(TEACH_DP, None), P(), P(), P())
    return jax.shard_map(body, mesh=finer, in_specs=in_specs, out_specs=out_specs, check_vma=False)
```

time: 111 us -> 80.2 us (0.72)
  local copies, waits for them, and re-layouts: 28.5 us -> 4.19 us
  starting transfers between devices: 12 us -> 0 us
  Pallas kernels: 66 us -> 72.8 us
    unnamed x7 -> x3, local copies, waits for them, and re-layouts: 22.4 us -> 4.19 us
    all_to_all x1 -> x0, starting transfers between devices: 12 us -> none  [body(): lax.all_to_all(student_hidden, DP, split_axis=0, concat_axis=0, tiled=True)]
    pallas_call x1, Pallas kernels: 66 us -> 72.8 us  [distill(): pl.pallas_call(step_kernel, out_shape=(jax.ShapeDtypeStruct((8, VOCAB), F...]
    all_to_all x2 -> x0, local copies, waits for them, and re-layouts: 3.03 us -> none  [body(): lax.all_to_all(student_hidden, DP, split_axis=0, concat_axis=0, tiled=True)]
    pad x2 -> x0, local copies, waits for them, and re-layouts: 1.36 us -> none  [the longest x1 0.75 us: body(): tail = jnp.pad(out_weight[:, TAIL:], ((0, 0), (0, 2 * HALF_V - VOCAB)))]
  transfers between devices with their start and end apart: 1 -> 0, of which waited for: 0 -> 0; matrix products, arithmetic and copies ran while one was open for 20% -> 0% of each run, Pallas kernels for 0% -> 0%
where the time goes in v3:
time: 80.2 us; the launch traced here: 79.9 us
  Pallas kernels  72.8 us (91%)
  local copies, waits for them, and re-layouts  4.19 us (5%)
  between operations  2.98 us (4%)
    pallas_call x1, Pallas kernels, distill(): pl.pallas_call(step_kernel, out_shape=(jax.ShapeDtypeStruct((8, VOCAB), F...  72.8 us
    unnamed x3, local copies, waits for them, and re-layouts  4.19 us

profile of v3, /device:TPU:1, one launch (start us, length us, event | category | flops | bytes accessed | tf_op | source)
XLA Modules:
  0.0 79.9 jit_solution(13903436576712751793)
XLA Ops:
  1.3 72.8 %shard_map.120 = (f32[8,5000]{1,0:T(8,128)}, f32[1,1024]{1,0:T(1,128)}, f32[1,5000]{1,0:T(1,128)}, f32[1,128]{1,0:T(1,128)}) custom-call(bf16[5000,256]{1,0:T(8,128)(2,1)} %bitcast.16, bf16[5000,1024]{1,0:T(8,128)(2,1)} %bitcast.15, bf16[256,1024]{1,0:T(8,128)(2,1)} %hidden_ref.1, s32[1,256]{1,0:T(1,128)} %bitcast.21, s32[1,256]{1,0:T(1,128)} %bitcast.22, ...), custom_call_target="tpu_custom_call" | custom-call | tf_op jit(solution)/shard_map/pallas_call | solution.py:507
  74.1 1.6 %copy.18 = f32[8,5000]{1,0:T(8,128)} copy(f32[8,5000]{1,0:T(8,128)} %get-tuple-element.16) | data formatting | bytes 320000
  75.7 1.3 %copy.19 = f32[1024]{0:T(1024)} copy(f32[1024]{0:T(1024)} %bitcast.20) | data formatting | bytes 8192
  76.9 1.3 %copy.20 = f32[5000]{0:T(1024)} copy(f32[5000]{0:T(1024)} %bitcast.18) | data formatting | bytes 40000

commit v4 on v3

--- a/solution.py
+++ b/solution.py
@@ -23,13 +23,19 @@
 BLOCKS = 5
 THIRDS = ((0, 896), (896, 896), (1792, 768))
 WIDEST = 896
-STAGE_ROWS = (256, 128, 64, 32, 16, 8)
-STAGE_AT = (0, 256, 384, 0, 32, 48)
+CHUNKS = (((0, 512), (512, 384)), ((0, 512), (512, 384)), ((0, 384), (384, 384)))
+STAGE_ROWS = (256, 128, 64, 32)
+STAGE_AT = (0, 256, 384, 0)
 NARROW = 3
 NARROW_ROWS = 448
 WIDE_ROWS = 56
+LAST_AT = 32
+FLIPS = ((1, 0), (0, 1), (1, 1))
 PARTS = 6
-STAGES = 6
+STAGES = 4
+COPIES = 7
+ORDER = (0, 3, 1, 4, 2, 5)
+BITS = 6
 VEC = WIDTH + HALF_V + 128
 LOSS_AT = WIDTH + HALF_V
 STEP = 64
@@ -81,10 +87,11 @@
     place = [lax.axis_index(axis) for axis in DP]
     me = place[0] * 16 + place[1] * 4 + place[2]
 
-    def partner(bit):
+    def partner(*bits):
         ids = list(place)
-        v = place[bit % 3]
-        ids[bit % 3] = (3 - v) if bit >= 3 else (v + 1 - 2 * (v % 2))
+        for bit in bits:
+            v = place[bit % 3]
+            ids[bit % 3] = (3 - v) if bit >= 3 else (v + 1 - 2 * (v % 2))
         return (t, ids[0], ids[1], ids[2])
 
     def my_bit(bit):
@@ -95,25 +102,23 @@
     mine = [my_bit(bit) for bit in range(6)]
     other_core = (1 - t, place[0], place[1], place[2])
 
+    turned_by = [[(v + d) % 4 for d in range(4)] for v in place]
+
     def moved(k, sign):
         step = (k * 21) % CHIPS
         steps = (step // 16, (step // 4) % 4, step % 4)
-        return [(v + 4 + sign * s) % 4 for v, s in zip(place, steps)]
+        return [turned_by[axis][(sign * d) % 4] for axis, d in enumerate(steps)]
 
     def index_of(ids):
         return ids[0] * 16 + ids[1] * 4 + ids[2]
 
     barrier = pltpu.get_barrier_semaphore()
-    pl.semaphore_signal(barrier, inc=1, device_id=other_core, device_id_type=MESH)
-
-    def greet(k, carry):
+    for k in range(1, CHIPS):
         ids = moved(k, 1)
         pl.semaphore_signal(
             barrier, inc=1, device_id=(t, ids[0], ids[1], ids[2]), device_id_type=MESH
         )
-        return carry
-
-    lax.fori_loop(1, CHIPS, greet, 0)
+    pl.semaphore_signal(barrier, inc=1, device_id=other_core, device_id_type=MESH)
 
     cuts = (0, 1280, 2560, 3840, VOCAB)
     teacher_copies = [
@@ -171,6 +176,23 @@
     lax.fori_loop(0, ROWS // 16, pack, 0)
     arrived[me] = message[me]
 
+    pl.semaphore_wait(barrier, CHIPS)
+
+    def hidden_copy(k, receiving):
+        ids = moved(k, 1)
+        source = index_of(moved(k, -1)) if receiving else me
+        return pltpu.make_async_remote_copy(
+            src_ref=message.at[index_of(ids)],
+            dst_ref=arrived.at[source],
+            send_sem=hidden_send.at[k],
+            recv_sem=hidden_recv.at[k],
+            device_id=(t, ids[0], ids[1], ids[2]),
+            device_id_type=MESH,
+        )
+
+    for k in range(1, CHIPS):
+        hidden_copy(k, False).start()
+
     routes_row = routes_ref[...].astype(F32)
     live = (lane_ids(1, ROWS) < length_ref[...]).astype(F32)
     half_live = live * 0.5
@@ -201,26 +223,6 @@
     total = lax.fori_loop(0, 2 * HALF_V // STEP, sum_step, jnp.zeros((8, ROWS), F32), unroll=2)
     scale_row = weight_row / jnp.sum(total, axis=0, keepdims=True)
 
-    pl.semaphore_wait(barrier, CHIPS)
-
-    def hidden_copy(k, receiving):
-        ids = moved(k, 1)
-        source = index_of(moved(k, -1)) if receiving else me
-        return pltpu.make_async_remote_copy(
-            src_ref=message.at[index_of(ids)],
-            dst_ref=arrived.at[source],
-            send_sem=hidden_send.at[k],
-            recv_sem=hidden_recv.at[k],
-            device_id=(t, ids[0], ids[1], ids[2]),
-            device_id_type=MESH,
-        )
-
-    def send_hidden(k, carry):
-        hidden_copy(k, False).start()
-        return carry
-
-    lax.fori_loop(1, CHIPS, send_hidden, 0)
-
     target_row = target_ref[...]
     step_rows = sublane_ids(STEP, ROWS)
 
@@ -263,11 +265,8 @@
 
     lax.fori_loop(0, HALF_V // 128, bias_step, 0)
 
-    def wait_hidden(k, carry):
+    for k in range(1, CHIPS):
         hidden_copy(k, True).wait_recv()
-        return carry
-
-    lax.fori_loop(1, CHIPS, wait_hidden, 0)
     rows_in = arrived[...].reshape(CHIPS * 8, 512)
     for i in range(2):
         pick = (wanted + 4.0 * i == lane_ids(ROWS, CHIPS * 8).astype(F32)).astype(F32).astype(BF16)
@@ -356,46 +355,68 @@
         grad[rows, :] = (mass * jnp.exp(log_probs) - both).astype(BF16)
         return loss - folded(both * log_probs, 8, jnp.add)
 
-    def copy_of(part, stage):
-        width = THIRDS[part % 3][1]
+    def columns(part, chunk):
+        first, width = CHUNKS[part % 3][chunk]
+        return slice(first, first + width)
+
+    def grad_columns(part, chunk):
+        first = THIRDS[part % 3][0]
+        at = columns(part, chunk)
+        return slice(first + at.start, first + at.stop)
+
+    def remote(part, chunk, source, target, rows, index, device):
+        at = columns(part, chunk)
+        number = (part * 2 + chunk) * COPIES + index
+        return pltpu.make_async_remote_copy(
+            src_ref=source.at[part, rows, at],
+            dst_ref=target.at[part, rows, at],
+            send_sem=send_sem.at[number],
+            recv_sem=recv_sem.at[number],
+            device_id=device,
+            device_id_type=MESH,
+        )
+
+    def copy_of(part, chunk, stage):
         rows = slice(STAGE_AT[stage], STAGE_AT[stage] + STAGE_ROWS[stage])
         source, target = (sent, got) if stage < NARROW else (sent_wide, got_wide)
+        return remote(part, chunk, source, target, rows, stage, partners[(part + stage) % 6])
+
+    def last_copy(part, chunk, flip):
+        rows = slice(LAST_AT + 8 * flip, LAST_AT + 8 * flip + 8)
+        bits = [(part + STAGES + k) % 6 for k in range(2) if FLIPS[flip][k]]
+        return remote(part, chunk, sent_wide, got_wide, rows, STAGES + flip, partner(*bits))
+
+    def vec_copy(step):
         return pltpu.make_async_remote_copy(
-            src_ref=source.at[part, rows, 0:width],
-            dst_ref=target.at[part, rows, 0:width],
-            send_sem=send_sem.at[part * STAGES + stage],
-            recv_sem=recv_sem.at[part * STAGES + stage],
-            device_id=partners[(part + stage) % 6],
+            src_ref=vec.at[step],
+            dst_ref=vec_in.at[step],
+            send_sem=vec_send_sem.at[step],
+            recv_sem=vec_recv_sem.at[step],
+            device_id=partners[step] if step < BITS else other_core,
             device_id_type=MESH,
         )
 
-    def vec_copy(stage):
-        return pltpu.make_async_remote_copy(
-            src_ref=vec.at[stage],
-            dst_ref=vec_in.at[stage],
-            send_sem=vec_send_sem.at[stage],
-            recv_sem=vec_recv_sem.at[stage],
-            device_id=partners[stage] if stage < STAGES else other_core,
-            device_id_type=MESH,
-        )
-
-    def product(part, at):
-        first, width = THIRDS[part % 3]
+    def vec_step(step):
+        vec_copy(step - 1).wait_recv()
+        vec[step] = vec[step - 1] + vec_in[step - 1]
+        vec_copy(step).start()
+
+    def product(part, chunk, at):
         return lax.dot_general(
-            lhs[part, pl.ds(pl.multiple_of(at, 256), 256), :], grad[first:first + width, :],
+            lhs[part, pl.ds(pl.multiple_of(at, 256), 256), :], grad[grad_columns(part, chunk), :],
             (((1,), (1,)), ((), ())), preferred_element_type=F32,
         )
 
     loss = jnp.zeros((8, ROWS), F32)
-    for third in range(3):
-        first, width = THIRDS[third]
-        loss = lax.fori_loop(first // STEP, (first + width) // STEP, grad_step, loss)
-        for part in (third, third + 3):
-            sent[part, 0:256, 0:width] = product(part, (1 - mine[part]) * 256).astype(BF16)
-            copy_of(part, 0).start()
-
-    for part in range(PARTS):
-        acc[part, :, 0:THIRDS[part % 3][1]] = product(part, mine[part] * 256)
+    for chunk in range(2):
+        for third in range(3):
+            at = grad_columns(third, chunk)
+            loss = lax.fori_loop(at.start // STEP, at.stop // STEP, grad_step, loss)
+            for part in (third, third + 3):
+                block = product(part, chunk, (1 - mine[part]) * 256)
+                sent[part, 0:256, columns(part, chunk)] = block.astype(BF16)
+                copy_of(part, chunk, 0).start()
+
     for i in range(BLOCKS):
         at = slice(i * BLOCK_V, (i + 1) * BLOCK_V)
         grad_n[:, at] = jnp.transpose(grad[at, :].astype(F32)).astype(BF16)
@@ -409,55 +430,80 @@
     loss_here = jnp.sum(jnp.sum(loss, axis=0, keepdims=True), axis=1, keepdims=True)
     vec[0, :, LOSS_AT:VEC] = jnp.where(lane == 0, loss_here, jnp.where(lane == 1, frames_here, 0.0))
     vec_copy(0).start()
+    for chunk in range(2):
+        for part in ORDER:
+            acc[part, :, columns(part, chunk)] = product(part, chunk, mine[part] * 256)
+    for k in range(1, CHIPS):
+        hidden_copy(k, False).wait_send()
+    hidden_swap.wait_send()
+    stats_swap.wait_send()
+    for copy in soft_copies:
+        copy.wait_send()
 
     base = [0] * PARTS
     for stage in range(1, STAGES):
         rows = STAGE_ROWS[stage]
         before_at = STAGE_AT[stage - 1]
         incoming = got if stage - 1 < NARROW else got_wide
-        for part in (0, 3, 1, 4, 2, 5):
-            width = THIRDS[part % 3][1]
-            bit = mine[(part + stage) % 6]
-            away, stay = (1 - bit) * rows, bit * rows
-            unit = min(rows, 16)
-
-            def joined(offset):
-                at = pl.multiple_of(base[part] + offset, unit)
-                return acc[part, pl.ds(at, rows), 0:width] + incoming[
-                    part, pl.ds(pl.multiple_of(before_at + offset, unit), rows), 0:width
-                ].astype(F32)
-
-            copy_of(part, stage - 1).wait_recv()
-            block = joined(away)
-            place_at = slice(STAGE_AT[stage], STAGE_AT[stage] + rows)
-            if stage < NARROW:
-                sent[part, place_at, 0:width] = block.astype(BF16)
-            else:
-                sent_wide[part, place_at, 0:width] = block
-            copy_of(part, stage).start()
-            acc[part, pl.ds(pl.multiple_of(base[part] + stay, unit), rows), 0:width] = joined(stay)
-            base[part] = base[part] + stay
-        vec_copy(stage - 1).wait_recv()
-        vec[stage] = vec[stage - 1] + vec_in[stage - 1]
-        vec_copy(stage).start()
-
-    vec_copy(STAGES - 1).wait_recv()
-    vec[STAGES] = vec[STAGES - 1] + vec_in[STAGES - 1]
-    vec_copy(STAGES).start()
-    inverse = 1.0 / vec[STAGES, :, LOSS_AT + 1:LOSS_AT + 2]
-    for part in range(PARTS):
-        first, width = THIRDS[part % 3]
-        copy_of(part, STAGES - 1).wait_recv()
-        at = pl.multiple_of(base[part], 8)
-        final[part // 3, :, first:first + width] = (
-            acc[part, pl.ds(at, 8), 0:width]
-            + got_wide[part, STAGE_AT[-1]:STAGE_AT[-1] + 8, 0:width]
-        ) * inverse
+        for chunk in range(2):
+            if 2 * stage + chunk - 1 < BITS:
+                vec_step(2 * stage + chunk - 1)
+            for part in ORDER:
+                bit = mine[(part + stage) % 6]
+                away, stay = (1 - bit) * rows, bit * rows
+                at = columns(part, chunk)
+
+                def joined(offset):
+                    first = pl.multiple_of(base[part] + offset, 16)
+                    return acc[part, pl.ds(first, rows), at] + incoming[
+                        part, pl.ds(pl.multiple_of(before_at + offset, 16), rows), at
+                    ].astype(F32)
+
+                copy_of(part, chunk, stage - 1).wait_recv()
+                block = joined(away)
+                place_at = slice(STAGE_AT[stage], STAGE_AT[stage] + rows)
+                if stage < NARROW:
+                    sent[part, place_at, at] = block.astype(BF16)
+                else:
+                    sent_wide[part, place_at, at] = block
+                copy_of(part, chunk, stage).start()
+                acc[part, pl.ds(pl.multiple_of(base[part] + stay, 16), rows), at] = joined(stay)
+        for part in range(PARTS):
+            base[part] = base[part] + mine[(part + stage) % 6] * rows
+
+    for chunk in range(2):
+        for part in ORDER:
+            at = columns(part, chunk)
+            rows = pl.ds(pl.multiple_of(base[part], 32), 32)
+            high, low_bit = mine[(part + STAGES) % 6], mine[(part + STAGES + 1) % 6]
+            copy_of(part, chunk, STAGES - 1).wait_recv()
+            acc[part, rows, at] += got_wide[part, 0:32, at]
+            for flip in (2, 0, 1):
+                to_high = 1 - high if FLIPS[flip][0] else high
+                to_low = 1 - low_bit if FLIPS[flip][1] else low_bit
+                first = pl.multiple_of(base[part] + to_high * 16 + to_low * 8, 8)
+                sent_wide[part, LAST_AT + 8 * flip:LAST_AT + 8 * flip + 8, at] = acc[
+                    part, pl.ds(first, 8), at
+                ]
+                last_copy(part, chunk, flip).start()
+        if chunk == 0:
+            vec_step(BITS)
+    inverse = 1.0 / vec[BITS, :, LOSS_AT + 1:LOSS_AT + 2]
+    for chunk in range(2):
+        for part in ORDER:
+            at = columns(part, chunk)
+            high, low_bit = mine[(part + STAGES) % 6], mine[(part + STAGES + 1) % 6]
+            first = pl.multiple_of(base[part] + high * 16 + low_bit * 8, 8)
+            total = acc[part, pl.ds(first, 8), at]
+            for flip in range(3):
+                last_copy(part, chunk, flip).wait_recv()
+                total = total + got_wide[part, LAST_AT + 8 * flip:LAST_AT + 8 * flip + 8, at]
+            final[part // 3, :, grad_columns(part, chunk)] = total * inverse
 
     swap = to_pair(final.at[1 - t], final_in, 2)
     swap.start()
-    vec_copy(STAGES).wait_recv()
-    total, beside = vec[STAGES], vec_in[STAGES]
+    vec_copy(BITS).wait_recv()
+    total, beside = vec[BITS], vec_in[BITS]
     gain_out[...] = (total[:, 0:WIDTH] + beside[:, 0:WIDTH]) * inverse
     loss_out[...] = (total[:, LOSS_AT:VEC] + beside[:, LOSS_AT:VEC]) * inverse
 
@@ -473,6 +519,14 @@
         bias_out[:, HALF_V:VOCAB] = total[:, WIDTH:WIDTH + rest] * inverse
         weight_out[:, HALF_V:VOCAB] = final[1, :, 0:rest]
 
+    for part in range(PARTS):
+        for chunk in range(2):
+            for stage in range(STAGES):
+                copy_of(part, chunk, stage).wait_send()
+            for flip in range(3):
+                last_copy(part, chunk, flip).wait_send()
+    for step in range(BITS + 1):
+        vec_copy(step).wait_send()
     swap.wait_recv()
 
     @pl.when(t == 0)
@@ -483,21 +537,14 @@
     def _():
         weight_out[:, 0:HALF_V] = final_in[...]
 
-    def sent_hidden(k, carry):
-        hidden_copy(k, False).wait_send()
-        return carry
-
-    lax.fori_loop(1, CHIPS, sent_hidden, 0)
-    hidden_swap.wait_send()
-    stats_swap.wait_send()
     swap.wait_send()
-    for copy in soft_copies:
-        copy.wait_send()
-    for part in range(PARTS):
-        for stage in range(STAGES):
-            copy_of(part, stage).wait_send()
-    for stage in range(STAGES + 1):
-        vec_copy(stage).wait_send()
+
+
+def finish_kernel(weight_in, gain_in, bias_in, loss_in, weight_out, gain_out, bias_out, loss_out):
+    weight_out[...] = weight_in[...]
+    gain_out[...] = gain_in[...]
+    bias_out[...] = bias_in[...]
+    loss_out[...] = loss_in[...]
 
 
 def distill(teacher, weight, *small):
@@ -541,8 +588,8 @@
             pltpu.VMEM((PARTS, WIDE_ROWS, WIDEST), F32),
             pltpu.VMEM((2, 8, HALF_V), F32),
             pltpu.VMEM((8, HALF_V), F32),
-            pltpu.VMEM((STAGES + 1, 1, VEC), F32),
-            pltpu.VMEM((STAGES + 1, 1, VEC), F32),
+            pltpu.VMEM((BITS + 1, 1, VEC), F32),
+            pltpu.VMEM((BITS + 1, 1, VEC), F32),
             dma((PIECES,)),
             dma((BLOCKS,)),
             dma((CHIPS,)),
@@ -551,10 +598,10 @@
             dma((PIECES,)),
             dma((3,)),
             dma((3,)),
-            dma((PARTS * STAGES,)),
-            dma((PARTS * STAGES,)),
-            dma((STAGES + 1,)),
-            dma((STAGES + 1,)),
+            dma((PARTS * 2 * COPIES,)),
+            dma((PARTS * 2 * COPIES,)),
+            dma((BITS + 1,)),
+            dma((BITS + 1,)),
         ],
         compiler_params=pltpu.CompilerParams(
             collective_id=0, has_side_effects=True, vmem_limit_bytes=60 * 1024 * 1024
@@ -576,6 +623,14 @@
         out_bias[None],
         gain[None],
     )
+    vmem = pl.BlockSpec(memory_space=pltpu.VMEM)
+    parts = (weight_grad, gain_grad, bias_grad, loss)
+    weight_grad, gain_grad, bias_grad, loss = pl.pallas_call(
+        finish_kernel,
+        out_shape=tuple(jax.ShapeDtypeStruct(x.shape, x.dtype) for x in parts),
+        in_specs=[vmem] * 4,
+        out_specs=(vmem,) * 4,
+    )(*parts)
     return (weight_grad, gain_grad[0], bias_grad[0], loss[0, 0])
 
 

time: 80.2 us -> 69.8 us (0.87)
  Pallas kernels: 72.8 us -> 68.3 us
  local copies, waits for them, and re-layouts: 4.19 us -> 0 us
  between operations: 2.98 us -> 1.29 us
    pallas_call x1, Pallas kernels: 72.8 us -> 66.7 us  [distill(): pl.pallas_call(step_kernel, out_shape=(jax.ShapeDtypeStruct((8, VOCAB), F...]
    unnamed x3 -> x0, local copies, waits for them, and re-layouts: 4.19 us -> none
    pallas_call x0 -> x1, Pallas kernels: none -> 1.61 us  [body(): pl.pallas_call(finish_kernel, out_shape=tuple((jax.ShapeDtypeStruct(x.sha...]
where the time goes in v4:
time: 69.8 us; the launch traced here: 69.6 us
  Pallas kernels  68.3 us (98%)
  between operations  1.29 us (2%)
    pallas_call x1, Pallas kernels, distill(): pl.pallas_call(step_kernel, out_shape=(jax.ShapeDtypeStruct((8, VOCAB), F...  66.7 us
    pallas_call x1, Pallas kernels, body(): pl.pallas_call(finish_kernel, out_shape=tuple((jax.ShapeDtypeStruct(x.sha...  1.61 us

profile of v4, /device:TPU:1, one launch (start us, length us, event | category | flops | bytes accessed | tf_op | source)
XLA Modules:
  0.0 69.6 jit_solution(17717769954323961761)
XLA Ops:
  1.3 66.7 %shard_map.120 = (f32[8,5000]{1,0:T(8,128)}, f32[1,1024]{1,0:T(1,128)}, f32[1,5000]{1,0:T(1,128)}, f32[1,128]{1,0:T(1,128)}) custom-call(bf16[5000,256]{1,0:T(8,128)(2,1)} %bitcast.16, bf16[5000,1024]{1,0:T(8,128)(2,1)} %bitcast.15, bf16[256,1024]{1,0:T(8,128)(2,1)} %hidden_ref.1, s32[1,256]{1,0:T(1,128)} %bitcast.19, s32[1,256]{1,0:T(1,128)} %bitcast.20, ...), custom_call_target="tpu_custom_call" | custom-call | tf_op jit(solution)/shard_map/pallas_call | solution.py:554
  68.0 1.6 %shard_map.121 = (f32[8,5000]{1,0:T(8,128)}, f32[1,1024]{1,0:T(1,128)}, f32[1,5000]{1,0:T(1,128)}, f32[1,128]{1,0:T(1,128)}) custom-call(f32[8,5000]{1,0:T(8,128)} %get-tuple-element.12.weight_in, f32[1,1024]{1,0:T(1,128)} %get-tuple-element.13.gain_in, f32[1,5000]{1,0:T(1,128)} %get-tuple-element.14.bias_in, f32[1,128]{1,0:T(1,128)} %get-tuple-element.15.loss_in), custom_call_target="tpu_custom_call" | custom-call | tf_op jit(solution)/shard_map/pallas_call | solution.py:628

commit v5 on v4

--- a/solution.py
+++ b/solution.py
@@ -75,12 +75,13 @@
 
 
 def step_kernel(
-    teacher_hbm, weight_hbm, hidden_ref, routes_ref, agree_ref, target_ref, length_ref, bias_ref, gain_ref,
+    teacher_hbm, weight_hbm, hidden_hbm, routes_hbm, agree_hbm, target_hbm, bias_hbm, gain_hbm, length_ref,
     weight_out, gain_out, bias_out, loss_out,
+    hidden_ref, routes_ref, agree_ref, target_ref, gain_ref, bias_ref,
     teacher, soft, soft_in, weight, message, arrived, stats, stats_in, mine_h, their_h,
     bias_row, bias_t, normed, scaled, scaled_t, logits, grad, grad_n,
     lhs, acc, sent, got, sent_wide, got_wide, final, final_in, vec, vec_in,
-    teacher_sem, weight_sem, hidden_send, hidden_recv, soft_send, soft_recv, pair_send, pair_recv,
+    small_sem, teacher_sem, weight_sem, hidden_send, hidden_recv, soft_send, soft_recv, pair_send, pair_recv,
     send_sem, recv_sem, vec_send_sem, vec_recv_sem,
 ):
     t = lax.axis_index("teach")
@@ -112,6 +113,21 @@
     def index_of(ids):
         return ids[0] * 16 + ids[1] * 4 + ids[2]
 
+    small_copies = [
+        pltpu.make_async_copy(source, target, small_sem.at[i])
+        for i, (source, target) in enumerate(
+            (
+                (hidden_hbm, hidden_ref),
+                (routes_hbm, routes_ref),
+                (agree_hbm, agree_ref),
+                (target_hbm, target_ref),
+                (gain_hbm, gain_ref),
+                (bias_hbm, bias_ref),
+            )
+        )
+    ]
+    for copy in small_copies:
+        copy.start()
     barrier = pltpu.get_barrier_semaphore()
     for k in range(1, CHIPS):
         ids = moved(k, 1)
@@ -164,6 +180,8 @@
         weight[rest:HALF_V, :] = jnp.zeros((HALF_V - rest, WIDTH), BF16)
 
     low = sublane_ids(8, 512) < 4
+    for copy in small_copies:
+        copy.wait()
 
     def pack(k, carry):
         x = hidden_ref[pl.ds(pl.multiple_of(k * 16, 16), 16), :].astype(F32)
@@ -175,6 +193,40 @@
 
     lax.fori_loop(0, ROWS // 16, pack, 0)
     arrived[me] = message[me]
+
+    routes_row = routes_ref[...].astype(F32)
+    live = (lane_ids(1, ROWS) < length_ref[0]).astype(F32)
+    half_live = live * 0.5
+    weight_row = half_live * agree_ref[...].astype(F32)
+    frames_here = jnp.sum(live, axis=1, keepdims=True)
+    named = (routes_row == sublane_ids(STUDENTS, ROWS).astype(F32)).astype(F32)
+    earlier = (sublane_ids(ROWS, ROWS) < lane_ids(ROWS, ROWS)).astype(F32)
+    before = jnp.dot(named.astype(BF16), earlier.astype(BF16), preferred_element_type=F32)
+    slot = jnp.sum(before * named, axis=0, keepdims=True)
+    wanted = (routes_row - (t * CHIPS).astype(F32)) * 8.0 + slot
+    wanted = jnp.transpose(jnp.broadcast_to(wanted, (8, ROWS)))[:, 0:1]
+
+    bias_row[:, 0:VOCAB] = bias_ref[...]
+    bias_row[:, VOCAB:2 * HALF_V] = jnp.zeros((1, 2 * HALF_V - VOCAB), F32)
+
+    def bias_step(k, carry):
+        strip = bias_row[:, pl.ds(pl.multiple_of(t * HALF_V + k * 128, 128), 128)]
+        bias_t[rows_at(k, 128), :] = jnp.transpose(jnp.broadcast_to(strip, (128, 128)))
+        return carry
+
+    lax.fori_loop(0, HALF_V // 128, bias_step, 0)
+
+    teacher[VOCAB:2 * HALF_V, :] = jnp.full((2 * HALF_V - VOCAB, ROWS), -1e30, BF16)
+
+    def max_step(k, top):
+        return jnp.maximum(top, folded(teacher[rows_at(k), :], 16, jnp.maximum))
+
+    top = jnp.full((16, ROWS), -1e30, BF16)
+    for q in range(PIECES):
+        teacher_copies[q].wait()
+        last = cuts[q + 1] // STEP if q < PIECES - 1 else 2 * HALF_V // STEP
+        top = lax.fori_loop(cuts[q] // STEP, last, max_step, top, unroll=2)
+    top = jnp.max(top.astype(F32), axis=0, keepdims=True)
 
     pl.semaphore_wait(barrier, CHIPS)
 
@@ -193,30 +245,6 @@
     for k in range(1, CHIPS):
         hidden_copy(k, False).start()
 
-    routes_row = routes_ref[...].astype(F32)
-    live = (lane_ids(1, ROWS) < length_ref[...]).astype(F32)
-    half_live = live * 0.5
-    weight_row = half_live * agree_ref[...].astype(F32)
-    frames_here = jnp.sum(live, axis=1, keepdims=True)
-    named = (routes_row == sublane_ids(STUDENTS, ROWS).astype(F32)).astype(F32)
-    earlier = (sublane_ids(ROWS, ROWS) < lane_ids(ROWS, ROWS)).astype(F32)
-    before = jnp.dot(named.astype(BF16), earlier.astype(BF16), preferred_element_type=F32)
-    slot = jnp.sum(before * named, axis=0, keepdims=True)
-    wanted = (routes_row - (t * CHIPS).astype(F32)) * 8.0 + slot
-    wanted = jnp.transpose(jnp.broadcast_to(wanted, (8, ROWS)))[:, 0:1]
-
-    teacher[VOCAB:2 * HALF_V, :] = jnp.full((2 * HALF_V - VOCAB, ROWS), -1e30, BF16)
-
-    def max_step(k, top):
-        return jnp.maximum(top, folded(teacher[rows_at(k), :], 16, jnp.maximum))
-
-    top = jnp.full((16, ROWS), -1e30, BF16)
-    for q in range(PIECES):
-        teacher_copies[q].wait()
-        last = cuts[q + 1] // STEP if q < PIECES - 1 else 2 * HALF_V // STEP
-        top = lax.fori_loop(cuts[q] // STEP, last, max_step, top, unroll=2)
-    top = jnp.max(top.astype(F32), axis=0, keepdims=True)
-
     def sum_step(k, total):
         return total + folded(jnp.exp(teacher[rows_at(k), :].astype(F32) - top), 8, jnp.add)
 
@@ -255,16 +283,6 @@
     mass = lax.fori_loop(first, first + HALF_V // STEP, soft_step, mass)
     mass = jnp.sum(mass, axis=0, keepdims=True)
 
-    bias_row[:, 0:VOCAB] = bias_ref[...]
-    bias_row[:, VOCAB:2 * HALF_V] = jnp.zeros((1, 2 * HALF_V - VOCAB), F32)
-
-    def bias_step(k, carry):
-        strip = bias_row[:, pl.ds(pl.multiple_of(t * HALF_V + k * 128, 128), 128)]
-        bias_t[rows_at(k, 128), :] = jnp.transpose(jnp.broadcast_to(strip, (128, 128)))
-        return carry
-
-    lax.fori_loop(0, HALF_V // 128, bias_step, 0)
-
     for k in range(1, CHIPS):
         hidden_copy(k, True).wait_recv()
     rows_in = arrived[...].reshape(CHIPS * 8, 512)
@@ -297,18 +315,19 @@
     scaled_t[...] = turned.reshape(WIDTH // 8, 8, ROWS)
     scaled[...] = turned.astype(BF16)
 
-    peak = jnp.full((8, ROWS), -1e30, F32)
+    for copy in weight_copies:
+        copy.wait()
+
+    @pl.when(t == 0)
+    def _():
+        last_first.wait()
+
+    @pl.when(t == 1)
+    def _():
+        last_second.wait()
+
+    peaks, sums = [], []
     for i in range(BLOCKS):
-        if i < BLOCKS - 1:
-            weight_copies[i].wait()
-        else:
-            @pl.when(t == 0)
-            def _():
-                last_first.wait()
-
-            @pl.when(t == 1)
-            def _():
-                last_second.wait()
         at = slice(i * BLOCK_V, (i + 1) * BLOCK_V)
         slope = bias_t[at, :]
         block = jnp.dot(weight[at, :], scaled[...], preferred_element_type=F32)
@@ -317,13 +336,19 @@
             inside = sublane_ids(BLOCK_V, ROWS) < VOCAB - i * BLOCK_V - t * HALF_V
             block = jnp.where(inside, block, -1e30)
         logits[at, :] = block
-        peak = jnp.maximum(peak, folded(block, 8, jnp.maximum))
-    peak = jnp.max(peak, axis=0, keepdims=True)
-
-    def lse_step(k, total):
-        return total + folded(jnp.exp(logits[rows_at(k), :] - peak), 8, jnp.add)
-
-    total = lax.fori_loop(0, HALF_V // STEP, lse_step, jnp.zeros((8, ROWS), F32), unroll=2)
+        peak = jnp.max(folded(block, 8, jnp.maximum), axis=0, keepdims=True)
+        total = jnp.zeros((8, ROWS), F32)
+        for k in range(BLOCK_V // STEP):
+            part_at = slice(i * BLOCK_V + k * STEP, i * BLOCK_V + (k + 1) * STEP)
+            total = total + folded(jnp.exp(logits[part_at, :] - peak), 8, jnp.add)
+        peaks.append(peak)
+        sums.append(total)
+    peak = peaks[0]
+    for other in peaks[1:]:
+        peak = jnp.maximum(peak, other)
+    total = jnp.zeros((8, ROWS), F32)
+    for other, terms in zip(peaks, sums):
+        total = total + terms * jnp.exp(other - peak)
     lse = peak + jnp.log(jnp.sum(total, axis=0, keepdims=True))
     stats[...] = jnp.concatenate([lse, mass, jnp.zeros((6, ROWS), F32)], axis=0)
     stats_swap = to_pair(stats, stats_in, 1)
@@ -348,7 +373,7 @@
     mass = mass + there[1:2, :]
 
     def grad_step(k, loss):
-        rows = rows_at(k)
+        rows = slice(k * STEP, (k + 1) * STEP)
         log_probs = logits[rows, :] - lse
         own = pl.ds(pl.multiple_of(t * HALF_V + k * STEP, STEP), STEP)
         both = soft[own, :].astype(F32) + soft_in[rows, :].astype(F32)
@@ -411,7 +436,8 @@
     for chunk in range(2):
         for third in range(3):
             at = grad_columns(third, chunk)
-            loss = lax.fori_loop(at.start // STEP, at.stop // STEP, grad_step, loss)
+            for k in range(at.start // STEP, at.stop // STEP):
+                loss = grad_step(k, loss)
             for part in (third, third + 3):
                 block = product(part, chunk, (1 - mine[part]) * 256)
                 sent[part, 0:256, columns(part, chunk)] = block.astype(BF16)
@@ -547,7 +573,7 @@
     loss_out[...] = loss_in[...]
 
 
-def distill(teacher, weight, *small):
+def distill(*arrays):
     vmem = pl.BlockSpec(memory_space=pltpu.VMEM)
     hbm = pl.BlockSpec(memory_space=pl.ANY)
     dma = pltpu.SemaphoreType.DMA
@@ -559,9 +585,15 @@
             jax.ShapeDtypeStruct((1, VOCAB), F32),
             jax.ShapeDtypeStruct((1, 128), F32),
         ),
-        in_specs=[hbm, hbm] + [vmem] * len(small),
+        in_specs=[hbm] * 8 + [pl.BlockSpec(memory_space=pltpu.SMEM)],
         out_specs=(vmem,) * 4,
         scratch_shapes=[
+            pltpu.VMEM((ROWS, WIDTH), BF16),
+            pltpu.VMEM((1, ROWS), jnp.int32),
+            pltpu.VMEM((1, ROWS), jnp.int32),
+            pltpu.VMEM((1, ROWS), jnp.int32),
+            pltpu.VMEM((1, WIDTH), F32),
+            pltpu.VMEM((1, VOCAB), F32),
             pltpu.VMEM((2 * HALF_V, ROWS), BF16),
             pltpu.VMEM((2 * HALF_V, ROWS), BF16),
             pltpu.VMEM((HALF_V, ROWS), BF16),
@@ -590,6 +622,7 @@
             pltpu.VMEM((8, HALF_V), F32),
             pltpu.VMEM((BITS + 1, 1, VEC), F32),
             pltpu.VMEM((BITS + 1, 1, VEC), F32),
+            dma((6,)),
             dma((PIECES,)),
             dma((BLOCKS,)),
             dma((CHIPS,)),
@@ -606,7 +639,7 @@
         compiler_params=pltpu.CompilerParams(
             collective_id=0, has_side_effects=True, vmem_limit_bytes=60 * 1024 * 1024
         ),
-    )(teacher, weight, *small)
+    )(*arrays)
 
 
 def body(
@@ -619,9 +652,9 @@
         routes.reshape(1, ROWS),
         agreement[None],
         targets[None],
-        lengths[None],
         out_bias[None],
         gain[None],
+        lengths,
     )
     vmem = pl.BlockSpec(memory_space=pltpu.VMEM)
     parts = (weight_grad, gain_grad, bias_grad, loss)

time: 69.8 us -> 66.8 us (0.957)
  Pallas kernels: 68.3 us -> 65.4 us
    pallas_call x1, Pallas kernels: 66.7 us -> 63.8 us  [distill(): pl.pallas_call(step_kernel, out_shape=(jax.ShapeDtypeStruct((8, VOCAB), F...]
where the time goes in v5:
time: 66.8 us; the launch traced here: 66.7 us
  Pallas kernels  65.4 us (98%)
  between operations  1.29 us (2%)
    pallas_call x1, Pallas kernels, distill(): pl.pallas_call(step_kernel, out_shape=(jax.ShapeDtypeStruct((8, VOCAB), F...  63.8 us
    pallas_call x1, Pallas kernels, body(): pl.pallas_call(finish_kernel, out_shape=tuple((jax.ShapeDtypeStruct(x.sha...  1.61 us

profile of v5, /device:TPU:1, one launch (start us, length us, event | category | flops | bytes accessed | tf_op | source)
XLA Modules:
  0.0 66.7 jit_solution(16168445689102390341)
XLA Ops:
  1.3 63.8 %shard_map.120 = (f32[8,5000]{1,0:T(8,128)}, f32[1,1024]{1,0:T(1,128)}, f32[1,5000]{1,0:T(1,128)}, f32[1,128]{1,0:T(1,128)}) custom-call(bf16[5000,256]{1,0:T(8,128)(2,1)} %bitcast.14, bf16[5000,1024]{1,0:T(8,128)(2,1)} %bitcast.13, bf16[256,1024]{1,0:T(8,128)(2,1)} %hidden_hbm.1, s32[1,256]{1,0:T(1,128)} %bitcast.17, s32[1,256]{1,0:T(1,128)} %bitcast.18, ...), custom_call_target="tpu_custom_call" | custom-call | tf_op jit(solution)/shard_map/pallas_call | solution.py:580
  65.0 1.6 %shard_map.121 = (f32[8,5000]{1,0:T(8,128)}, f32[1,1024]{1,0:T(1,128)}, f32[1,5000]{1,0:T(1,128)}, f32[1,128]{1,0:T(1,128)}) custom-call(f32[8,5000]{1,0:T(8,128)} %get-tuple-element.12.weight_in, f32[1,1024]{1,0:T(1,128)} %get-tuple-element.13.gain_in, f32[1,5000]{1,0:T(1,128)} %get-tuple-element.14.bias_in, f32[1,128]{1,0:T(1,128)} %get-tuple-element.15.loss_in), custom_call_target="tpu_custom_call" | custom-call | tf_op jit(solution)/shard_map/pallas_call | solution.py:661

commit v6 on v5

--- a/solution.py
+++ b/solution.py
@@ -35,7 +35,7 @@
 STAGES = 4
 COPIES = 7
 ORDER = (0, 3, 1, 4, 2, 5)
-BITS = 6
+ROUNDS = 3
 VEC = WIDTH + HALF_V + 128
 LOSS_AT = WIDTH + HALF_V
 STEP = 64
@@ -52,6 +52,13 @@
         low, high = bits[dim], bits[3 + dim]
         chip = chip * 4 + high * 2 + (high ^ low)
     return chip
+
+
+def hops(k):
+    return sum(min(d, 4 - d) for d in (k // 16, (k // 4) % 4, k % 4))
+
+
+OFFSETS = tuple(sorted(((k * 21) % CHIPS for k in range(1, CHIPS)), key=lambda k: -hops(k)))
 
 
 def rows_at(k, size=STEP):
@@ -106,8 +113,7 @@
     turned_by = [[(v + d) % 4 for d in range(4)] for v in place]
 
     def moved(k, sign):
-        step = (k * 21) % CHIPS
-        steps = (step // 16, (step // 4) % 4, step % 4)
+        steps = (k // 16, (k // 4) % 4, k % 4)
         return [turned_by[axis][(sign * d) % 4] for axis, d in enumerate(steps)]
 
     def index_of(ids):
@@ -129,7 +135,7 @@
     for copy in small_copies:
         copy.start()
     barrier = pltpu.get_barrier_semaphore()
-    for k in range(1, CHIPS):
+    for k in OFFSETS:
         ids = moved(k, 1)
         pl.semaphore_signal(
             barrier, inc=1, device_id=(t, ids[0], ids[1], ids[2]), device_id_type=MESH
@@ -242,7 +248,7 @@
             device_id_type=MESH,
         )
 
-    for k in range(1, CHIPS):
+    for k in OFFSETS:
         hidden_copy(k, False).start()
 
     def sum_step(k, total):
@@ -283,14 +289,9 @@
     mass = lax.fori_loop(first, first + HALF_V // STEP, soft_step, mass)
     mass = jnp.sum(mass, axis=0, keepdims=True)
 
-    for k in range(1, CHIPS):
+    for k in OFFSETS:
         hidden_copy(k, True).wait_recv()
     rows_in = arrived[...].reshape(CHIPS * 8, 512)
-    for i in range(2):
-        pick = (wanted + 4.0 * i == lane_ids(ROWS, CHIPS * 8).astype(F32)).astype(F32).astype(BF16)
-        mine_h[:, 512 * i:512 * i + 512] = jnp.dot(
-            pick, rows_in, preferred_element_type=F32
-        ).astype(BF16)
 
     def to_pair(source, target, index):
         return pltpu.make_async_remote_copy(
@@ -302,10 +303,16 @@
             device_id_type=MESH,
         )
 
-    hidden_swap = to_pair(mine_h, their_h, 0)
-    hidden_swap.start()
-
-    hidden_swap.wait_recv()
+    hidden_swaps = []
+    for i in range(2):
+        pick = (wanted + 4.0 * i == lane_ids(ROWS, CHIPS * 8).astype(F32)).astype(F32).astype(BF16)
+        at = slice(512 * i, 512 * i + 512)
+        mine_h[:, at] = jnp.dot(pick, rows_in, preferred_element_type=F32).astype(BF16)
+        hidden_swaps.append(to_pair(mine_h.at[:, at], their_h.at[:, at], 3 * i))
+        hidden_swaps[i].start()
+
+    for copy in hidden_swaps:
+        copy.wait_recv()
     states = mine_h[...].astype(F32) + their_h[...].astype(F32)
     states = states - jnp.mean(states, axis=1, keepdims=True)
     spread = jnp.mean(jnp.square(states), axis=1, keepdims=True)
@@ -411,20 +418,27 @@
         bits = [(part + STAGES + k) % 6 for k in range(2) if FLIPS[flip][k]]
         return remote(part, chunk, sent_wide, got_wide, rows, STAGES + flip, partner(*bits))
 
-    def vec_copy(step):
+    def vec_copy(step, flip):
+        bits = [2 * step + k for k in range(2) if FLIPS[flip][k]]
         return pltpu.make_async_remote_copy(
             src_ref=vec.at[step],
-            dst_ref=vec_in.at[step],
-            send_sem=vec_send_sem.at[step],
-            recv_sem=vec_recv_sem.at[step],
-            device_id=partners[step] if step < BITS else other_core,
+            dst_ref=vec_in.at[3 * step + flip],
+            send_sem=vec_send_sem.at[3 * step + flip],
+            recv_sem=vec_recv_sem.at[3 * step + flip],
+            device_id=partner(*bits) if step < ROUNDS else other_core,
             device_id_type=MESH,
         )
 
+    def vec_start(step):
+        for flip in (2, 0, 1) if step < ROUNDS else (0,):
+            vec_copy(step, flip).start()
+
     def vec_step(step):
-        vec_copy(step - 1).wait_recv()
-        vec[step] = vec[step - 1] + vec_in[step - 1]
-        vec_copy(step).start()
+        for flip in range(3):
+            vec_copy(step - 1, flip).wait_recv()
+        at = 3 * (step - 1)
+        vec[step] = (vec[step - 1] + vec_in[at]) + (vec_in[at + 1] + vec_in[at + 2])
+        vec_start(step)
 
     def product(part, chunk, at):
         return lax.dot_general(
@@ -455,13 +469,14 @@
     lane = lane_ids(1, 128)
     loss_here = jnp.sum(jnp.sum(loss, axis=0, keepdims=True), axis=1, keepdims=True)
     vec[0, :, LOSS_AT:VEC] = jnp.where(lane == 0, loss_here, jnp.where(lane == 1, frames_here, 0.0))
-    vec_copy(0).start()
+    vec_start(0)
     for chunk in range(2):
         for part in ORDER:
             acc[part, :, columns(part, chunk)] = product(part, chunk, mine[part] * 256)
-    for k in range(1, CHIPS):
+    for k in OFFSETS:
         hidden_copy(k, False).wait_send()
-    hidden_swap.wait_send()
+    for copy in hidden_swaps:
+        copy.wait_send()
     stats_swap.wait_send()
     for copy in soft_copies:
         copy.wait_send()
@@ -472,14 +487,13 @@
         before_at = STAGE_AT[stage - 1]
         incoming = got if stage - 1 < NARROW else got_wide
         for chunk in range(2):
-            if 2 * stage + chunk - 1 < BITS:
-                vec_step(2 * stage + chunk - 1)
+            kept = []
             for part in ORDER:
                 bit = mine[(part + stage) % 6]
                 away, stay = (1 - bit) * rows, bit * rows
                 at = columns(part, chunk)
 
-                def joined(offset):
+                def joined(offset, part=part, at=at):
                     first = pl.multiple_of(base[part] + offset, 16)
                     return acc[part, pl.ds(first, rows), at] + incoming[
                         part, pl.ds(pl.multiple_of(before_at + offset, 16), rows), at
@@ -493,7 +507,10 @@
                 else:
                     sent_wide[part, place_at, at] = block
                 copy_of(part, chunk, stage).start()
-                acc[part, pl.ds(pl.multiple_of(base[part] + stay, 16), rows), at] = joined(stay)
+                kept.append((part, at, pl.ds(pl.multiple_of(base[part] + stay, 16), rows), joined, stay))
+            for part, at, where, sum_at, stay in kept:
+                acc[part, where, at] = sum_at(stay)
+        vec_step(stage)
         for part in range(PARTS):
             base[part] = base[part] + mine[(part + stage) % 6] * rows
 
@@ -512,9 +529,7 @@
                     part, pl.ds(first, 8), at
                 ]
                 last_copy(part, chunk, flip).start()
-        if chunk == 0:
-            vec_step(BITS)
-    inverse = 1.0 / vec[BITS, :, LOSS_AT + 1:LOSS_AT + 2]
+    inverse = 1.0 / vec[ROUNDS, :, LOSS_AT + 1:LOSS_AT + 2]
     for chunk in range(2):
         for part in ORDER:
             at = columns(part, chunk)
@@ -528,8 +543,8 @@
 
     swap = to_pair(final.at[1 - t], final_in, 2)
     swap.start()
-    vec_copy(BITS).wait_recv()
-    total, beside = vec[BITS], vec_in[BITS]
+    vec_copy(ROUNDS, 0).wait_recv()
+    total, beside = vec[ROUNDS], vec_in[3 * ROUNDS]
     gain_out[...] = (total[:, 0:WIDTH] + beside[:, 0:WIDTH]) * inverse
     loss_out[...] = (total[:, LOSS_AT:VEC] + beside[:, LOSS_AT:VEC]) * inverse
 
@@ -551,8 +566,10 @@
                 copy_of(part, chunk, stage).wait_send()
             for flip in range(3):
                 last_copy(part, chunk, flip).wait_send()
-    for step in range(BITS + 1):
-        vec_copy(step).wait_send()
+    for step in range(ROUNDS):
+        for flip in range(3):
+            vec_copy(step, flip).wait_send()
+    vec_copy(ROUNDS, 0).wait_send()
     swap.wait_recv()
 
     @pl.when(t == 0)
@@ -620,8 +637,8 @@
             pltpu.VMEM((PARTS, WIDE_ROWS, WIDEST), F32),
             pltpu.VMEM((2, 8, HALF_V), F32),
             pltpu.VMEM((8, HALF_V), F32),
-            pltpu.VMEM((BITS + 1, 1, VEC), F32),
-            pltpu.VMEM((BITS + 1, 1, VEC), F32),
+            pltpu.VMEM((ROUNDS + 1, 1, VEC), F32),
+            pltpu.VMEM((3 * ROUNDS + 1, 1, VEC), F32),
             dma((6,)),
             dma((PIECES,)),
             dma((BLOCKS,)),
@@ -629,12 +646,12 @@
             dma((CHIPS,)),
             dma((PIECES,)),
             dma((PIECES,)),
-            dma((3,)),
-            dma((3,)),
+            dma((4,)),
+            dma((4,)),
             dma((PARTS * 2 * COPIES,)),
             dma((PARTS * 2 * COPIES,)),
-            dma((BITS + 1,)),
-            dma((BITS + 1,)),
+            dma((3 * ROUNDS + 1,)),
+            dma((3 * ROUNDS + 1,)),
         ],
         compiler_params=pltpu.CompilerParams(
             collective_id=0, has_side_effects=True, vmem_limit_bytes=60 * 1024 * 1024

time: 66.8 us -> 63.6 us (0.952)
  Pallas kernels: 65.4 us -> 62.2 us
    pallas_call x1, Pallas kernels: 63.8 us -> 60.6 us  [distill(): pl.pallas_call(step_kernel, out_shape=(jax.ShapeDtypeStruct((8, VOCAB), F...]
where the time goes in v6:
time: 63.6 us; the launch traced here: 63.5 us
  Pallas kernels  62.2 us (98%)
  between operations  1.29 us (2%)
    pallas_call x1, Pallas kernels, distill(): pl.pallas_call(step_kernel, out_shape=(jax.ShapeDtypeStruct((8, VOCAB), F...  60.6 us
    pallas_call x1, Pallas kernels, body(): pl.pallas_call(finish_kernel, out_shape=tuple((jax.ShapeDtypeStruct(x.sha...  1.61 us

profile of v6, /device:TPU:1, one launch (start us, length us, event | category | flops | bytes accessed | tf_op | source)
XLA Modules:
  0.0 63.5 jit_solution(10517850977312771970)
XLA Ops:
  1.3 60.6 %shard_map.120 = (f32[8,5000]{1,0:T(8,128)}, f32[1,1024]{1,0:T(1,128)}, f32[1,5000]{1,0:T(1,128)}, f32[1,128]{1,0:T(1,128)}) custom-call(bf16[5000,256]{1,0:T(8,128)(2,1)} %bitcast.14, bf16[5000,1024]{1,0:T(8,128)(2,1)} %bitcast.13, bf16[256,1024]{1,0:T(8,128)(2,1)} %hidden_hbm.1, s32[1,256]{1,0:T(1,128)} %bitcast.17, s32[1,256]{1,0:T(1,128)} %bitcast.18, ...), custom_call_target="tpu_custom_call" | custom-call | tf_op jit(solution)/shard_map/pallas_call | solution.py:597
  61.9 1.6 %shard_map.121 = (f32[8,5000]{1,0:T(8,128)}, f32[1,1024]{1,0:T(1,128)}, f32[1,5000]{1,0:T(1,128)}, f32[1,128]{1,0:T(1,128)}) custom-call(f32[8,5000]{1,0:T(8,128)} %get-tuple-element.12.weight_in, f32[1,1024]{1,0:T(1,128)} %get-tuple-element.13.gain_in, f32[1,5000]{1,0:T(1,128)} %get-tuple-element.14.bias_in, f32[1,128]{1,0:T(1,128)} %get-tuple-element.15.loss_in), custom_call_target="tpu_custom_call" | custom-call | tf_op jit(solution)/shard_map/pallas_call | solution.py:678

commit v7 on v6

--- a/solution.py
+++ b/solution.py
@@ -24,16 +24,16 @@
 THIRDS = ((0, 896), (896, 896), (1792, 768))
 WIDEST = 896
 CHUNKS = (((0, 512), (512, 384)), ((0, 512), (512, 384)), ((0, 384), (384, 384)))
-STAGE_ROWS = (256, 128, 64, 32)
-STAGE_AT = (0, 256, 384, 0)
-NARROW = 3
-NARROW_ROWS = 448
-WIDE_ROWS = 56
-LAST_AT = 32
+STAGE_ROWS = (256, 128)
+STAGE_AT = (0, 256)
+QUAD_ROWS = (32, 8)
+QUAD_AT = (384, 0)
+NARROW_ROWS = 480
+WIDE_ROWS = 24
 FLIPS = ((1, 0), (0, 1), (1, 1))
 PARTS = 6
-STAGES = 4
-COPIES = 7
+STAGES = 2
+COPIES = 8
 ORDER = (0, 3, 1, 4, 2, 5)
 ROUNDS = 3
 VEC = WIDTH + HALF_V + 128
@@ -410,13 +410,28 @@
 
     def copy_of(part, chunk, stage):
         rows = slice(STAGE_AT[stage], STAGE_AT[stage] + STAGE_ROWS[stage])
-        source, target = (sent, got) if stage < NARROW else (sent_wide, got_wide)
-        return remote(part, chunk, source, target, rows, stage, partners[(part + stage) % 6])
-
-    def last_copy(part, chunk, flip):
-        rows = slice(LAST_AT + 8 * flip, LAST_AT + 8 * flip + 8)
-        bits = [(part + STAGES + k) % 6 for k in range(2) if FLIPS[flip][k]]
-        return remote(part, chunk, sent_wide, got_wide, rows, STAGES + flip, partner(*bits))
+        return remote(part, chunk, sent, got, rows, stage, partners[(part + stage) % 6])
+
+    def quad_bits(part, turn):
+        first = part + STAGES + 2 * turn
+        return first % 6, (first + 1) % 6
+
+    def quad_rows(turn, flip):
+        first = QUAD_AT[turn] + QUAD_ROWS[turn] * flip
+        return slice(first, first + QUAD_ROWS[turn])
+
+    def quad_copy(part, chunk, turn, flip):
+        bits = [bit for bit, wanted in zip(quad_bits(part, turn), FLIPS[flip]) if wanted]
+        source, target = (sent, got) if turn == 0 else (sent_wide, got_wide)
+        index = STAGES + 3 * turn + flip
+        return remote(part, chunk, source, target, quad_rows(turn, flip), index, partner(*bits))
+
+    def quad_offset(part, turn, flip):
+        first, second = (mine[bit] for bit in quad_bits(part, turn))
+        if flip is not None:
+            first = 1 - first if FLIPS[flip][0] else first
+            second = 1 - second if FLIPS[flip][1] else second
+        return (first * 2 + second) * QUAD_ROWS[turn]
 
     def vec_copy(step, flip):
         bits = [2 * step + k for k in range(2) if FLIPS[flip][k]]
@@ -481,64 +496,68 @@
     for copy in soft_copies:
         copy.wait_send()
 
-    base = [0] * PARTS
-    for stage in range(1, STAGES):
-        rows = STAGE_ROWS[stage]
-        before_at = STAGE_AT[stage - 1]
-        incoming = got if stage - 1 < NARROW else got_wide
-        for chunk in range(2):
-            kept = []
-            for part in ORDER:
-                bit = mine[(part + stage) % 6]
-                away, stay = (1 - bit) * rows, bit * rows
-                at = columns(part, chunk)
-
-                def joined(offset, part=part, at=at):
-                    first = pl.multiple_of(base[part] + offset, 16)
-                    return acc[part, pl.ds(first, rows), at] + incoming[
-                        part, pl.ds(pl.multiple_of(before_at + offset, 16), rows), at
-                    ].astype(F32)
-
-                copy_of(part, chunk, stage - 1).wait_recv()
-                block = joined(away)
-                place_at = slice(STAGE_AT[stage], STAGE_AT[stage] + rows)
-                if stage < NARROW:
-                    sent[part, place_at, at] = block.astype(BF16)
-                else:
-                    sent_wide[part, place_at, at] = block
-                copy_of(part, chunk, stage).start()
-                kept.append((part, at, pl.ds(pl.multiple_of(base[part] + stay, 16), rows), joined, stay))
-            for part, at, where, sum_at, stay in kept:
-                acc[part, where, at] = sum_at(stay)
-        vec_step(stage)
-        for part in range(PARTS):
-            base[part] = base[part] + mine[(part + stage) % 6] * rows
-
+    def taken(part, at, first, rows, begin):
+        return acc[part, pl.ds(first, rows), at] + got[
+            part, pl.ds(pl.multiple_of(begin, 16), rows), at
+        ].astype(F32)
+
+    rows, base = STAGE_ROWS[1], [0] * PARTS
     for chunk in range(2):
         for part in ORDER:
             at = columns(part, chunk)
-            rows = pl.ds(pl.multiple_of(base[part], 32), 32)
-            high, low_bit = mine[(part + STAGES) % 6], mine[(part + STAGES + 1) % 6]
-            copy_of(part, chunk, STAGES - 1).wait_recv()
-            acc[part, rows, at] += got_wide[part, 0:32, at]
+            away = pl.multiple_of((1 - mine[(part + 1) % 6]) * rows, rows)
+            copy_of(part, chunk, 0).wait_recv()
+            sent[part, STAGE_AT[1]:STAGE_AT[1] + rows, at] = taken(part, at, away, rows, away).astype(BF16)
+            copy_of(part, chunk, 1).start()
+        for part in ORDER:
+            at = columns(part, chunk)
+            stay = pl.multiple_of(mine[(part + 1) % 6] * rows, rows)
+            acc[part, pl.ds(stay, rows), at] = taken(part, at, stay, rows, stay)
+    vec_step(1)
+    base = [mine[(part + 1) % 6] * rows for part in range(PARTS)]
+
+    rows = QUAD_ROWS[0]
+    for chunk in range(2):
+        for part in ORDER:
+            at = columns(part, chunk)
+            copy_of(part, chunk, 1).wait_recv()
             for flip in (2, 0, 1):
-                to_high = 1 - high if FLIPS[flip][0] else high
-                to_low = 1 - low_bit if FLIPS[flip][1] else low_bit
-                first = pl.multiple_of(base[part] + to_high * 16 + to_low * 8, 8)
-                sent_wide[part, LAST_AT + 8 * flip:LAST_AT + 8 * flip + 8, at] = acc[
-                    part, pl.ds(first, 8), at
-                ]
-                last_copy(part, chunk, flip).start()
+                offset = quad_offset(part, 0, flip)
+                first = pl.multiple_of(base[part] + offset, rows)
+                block = taken(part, at, first, rows, STAGE_AT[1] + offset)
+                sent[part, quad_rows(0, flip), at] = block.astype(BF16)
+                quad_copy(part, chunk, 0, flip).start()
+        for part in ORDER:
+            at = columns(part, chunk)
+            offset = quad_offset(part, 0, None)
+            first = pl.multiple_of(base[part] + offset, rows)
+            acc[part, pl.ds(first, rows), at] = taken(part, at, first, rows, STAGE_AT[1] + offset)
+    vec_step(2)
+    base = [base[part] + quad_offset(part, 0, None) for part in range(PARTS)]
+
+    for chunk in range(2):
+        for part in ORDER:
+            at = columns(part, chunk)
+            where = pl.ds(pl.multiple_of(base[part], rows), rows)
+            block = acc[part, where, at]
+            for flip in range(3):
+                quad_copy(part, chunk, 0, flip).wait_recv()
+                block = block + got[part, quad_rows(0, flip), at].astype(F32)
+            acc[part, where, at] = block
+            for flip in (2, 0, 1):
+                first = pl.multiple_of(base[part] + quad_offset(part, 1, flip), 8)
+                sent_wide[part, quad_rows(1, flip), at] = acc[part, pl.ds(first, 8), at]
+                quad_copy(part, chunk, 1, flip).start()
+    vec_step(3)
     inverse = 1.0 / vec[ROUNDS, :, LOSS_AT + 1:LOSS_AT + 2]
     for chunk in range(2):
         for part in ORDER:
             at = columns(part, chunk)
-            high, low_bit = mine[(part + STAGES) % 6], mine[(part + STAGES + 1) % 6]
-            first = pl.multiple_of(base[part] + high * 16 + low_bit * 8, 8)
+            first = pl.multiple_of(base[part] + quad_offset(part, 1, None), 8)
             total = acc[part, pl.ds(first, 8), at]
             for flip in range(3):
-                last_copy(part, chunk, flip).wait_recv()
-                total = total + got_wide[part, LAST_AT + 8 * flip:LAST_AT + 8 * flip + 8, at]
+                quad_copy(part, chunk, 1, flip).wait_recv()
+                total = total + got_wide[part, quad_rows(1, flip), at]
             final[part // 3, :, grad_columns(part, chunk)] = total * inverse
 
     swap = to_pair(final.at[1 - t], final_in, 2)
@@ -564,8 +583,9 @@
         for chunk in range(2):
             for stage in range(STAGES):
                 copy_of(part, chunk, stage).wait_send()
-            for flip in range(3):
-                last_copy(part, chunk, flip).wait_send()
+            for turn in range(2):
+                for flip in range(3):
+                    quad_copy(part, chunk, turn, flip).wait_send()
     for step in range(ROUNDS):
         for flip in range(3):
             vec_copy(step, flip).wait_send()

time: 63.6 us -> 61.6 us (0.969)
  Pallas kernels: 62.2 us -> 60.2 us
    pallas_call x1, Pallas kernels: 60.6 us -> 58.6 us  [distill(): pl.pallas_call(step_kernel, out_shape=(jax.ShapeDtypeStruct((8, VOCAB), F...]
where the time goes in v7:
time: 61.6 us; the launch traced here: 61.4 us
  Pallas kernels  60.2 us (98%)
  between operations  1.29 us (2%)
    pallas_call x1, Pallas kernels, distill(): pl.pallas_call(step_kernel, out_shape=(jax.ShapeDtypeStruct((8, VOCAB), F...  58.6 us
    pallas_call x1, Pallas kernels, body(): pl.pallas_call(finish_kernel, out_shape=tuple((jax.ShapeDtypeStruct(x.sha...  1.61 us

profile of v7, /device:TPU:1, one launch (start us, length us, event | category | flops | bytes accessed | tf_op | source)
XLA Modules:
  0.0 61.4 jit_solution(17981062873072872528)
XLA Ops:
  1.3 58.6 %shard_map.120 = (f32[8,5000]{1,0:T(8,128)}, f32[1,1024]{1,0:T(1,128)}, f32[1,5000]{1,0:T(1,128)}, f32[1,128]{1,0:T(1,128)}) custom-call(bf16[5000,256]{1,0:T(8,128)(2,1)} %bitcast.14, bf16[5000,1024]{1,0:T(8,128)(2,1)} %bitcast.13, bf16[256,1024]{1,0:T(8,128)(2,1)} %hidden_hbm.1, s32[1,256]{1,0:T(1,128)} %bitcast.17, s32[1,256]{1,0:T(1,128)} %bitcast.18, ...), custom_call_target="tpu_custom_call" | custom-call | tf_op jit(solution)/shard_map/pallas_call | solution.py:617
  59.8 1.6 %shard_map.121 = (f32[8,5000]{1,0:T(8,128)}, f32[1,1024]{1,0:T(1,128)}, f32[1,5000]{1,0:T(1,128)}, f32[1,128]{1,0:T(1,128)}) custom-call(f32[8,5000]{1,0:T(8,128)} %get-tuple-element.12.weight_in, f32[1,1024]{1,0:T(1,128)} %get-tuple-element.13.gain_in, f32[1,5000]{1,0:T(1,128)} %get-tuple-element.14.bias_in, f32[1,128]{1,0:T(1,128)} %get-tuple-element.15.loss_in), custom_call_target="tpu_custom_call" | custom-call | tf_op jit(solution)/shard_map/pallas_call | solution.py:698

commit v8 on v7

--- a/solution.py
+++ b/solution.py
@@ -470,7 +470,11 @@
             for part in (third, third + 3):
                 block = product(part, chunk, (1 - mine[part]) * 256)
                 sent[part, 0:256, columns(part, chunk)] = block.astype(BF16)
-                copy_of(part, chunk, 0).start()
+
+            @pl.when(t == 0)
+            def _(third=third, chunk=chunk):
+                for part in (third, third + 3):
+                    copy_of(part, chunk, 0).start()
 
     for i in range(BLOCKS):
         at = slice(i * BLOCK_V, (i + 1) * BLOCK_V)
@@ -485,6 +489,13 @@
     loss_here = jnp.sum(jnp.sum(loss, axis=0, keepdims=True), axis=1, keepdims=True)
     vec[0, :, LOSS_AT:VEC] = jnp.where(lane == 0, loss_here, jnp.where(lane == 1, frames_here, 0.0))
     vec_start(0)
+
+    @pl.when(t == 1)
+    def _():
+        for chunk in range(2):
+            for part in ORDER:
+                copy_of(part, chunk, 0).start()
+
     for chunk in range(2):
         for part in ORDER:
             acc[part, :, columns(part, chunk)] = product(part, chunk, mine[part] * 256)

time: 61.6 us -> 61.1 us (level)
  no operation moved by 1% of the time
where the time goes in v8:
time: 61.1 us; the launch traced here: 61 us
  Pallas kernels  59.7 us (98%)
  between operations  1.29 us (2%)
    pallas_call x1, Pallas kernels, distill(): pl.pallas_call(step_kernel, out_shape=(jax.ShapeDtypeStruct((8, VOCAB), F...  58.1 us
    pallas_call x1, Pallas kernels, body(): pl.pallas_call(finish_kernel, out_shape=tuple((jax.ShapeDtypeStruct(x.sha...  1.61 us

profile of v8, /device:TPU:1, one launch (start us, length us, event | category | flops | bytes accessed | tf_op | source)
XLA Modules:
  0.0 61.0 jit_solution(9712942889600637849)
XLA Ops:
  1.3 58.1 %shard_map.120 = (f32[8,5000]{1,0:T(8,128)}, f32[1,1024]{1,0:T(1,128)}, f32[1,5000]{1,0:T(1,128)}, f32[1,128]{1,0:T(1,128)}) custom-call(bf16[5000,256]{1,0:T(8,128)(2,1)} %bitcast.14, bf16[5000,1024]{1,0:T(8,128)(2,1)} %bitcast.13, bf16[256,1024]{1,0:T(8,128)(2,1)} %hidden_hbm.1, s32[1,256]{1,0:T(1,128)} %bitcast.17, s32[1,256]{1,0:T(1,128)} %bitcast.18, ...), custom_call_target="tpu_custom_call" | custom-call | tf_op jit(solution)/shard_map/pallas_call | solution.py:628
  59.4 1.6 %shard_map.121 = (f32[8,5000]{1,0:T(8,128)}, f32[1,1024]{1,0:T(1,128)}, f32[1,5000]{1,0:T(1,128)}, f32[1,128]{1,0:T(1,128)}) custom-call(f32[8,5000]{1,0:T(8,128)} %get-tuple-element.12.weight_in, f32[1,1024]{1,0:T(1,128)} %get-tuple-element.13.gain_in, f32[1,5000]{1,0:T(1,128)} %get-tuple-element.14.bias_in, f32[1,128]{1,0:T(1,128)} %get-tuple-element.15.loss_in), custom_call_target="tpu_custom_call" | custom-call | tf_op jit(solution)/shard_map/pallas_call | solution.py:709
